TPU v7x, 512 devices: a whole 4x8x8 slice. The times are simulated.
512 devices in a mesh: blk: 32 (over y, z_hi, core), col: 16 (over x, z_lo).
Axes of the slice: x: 4, y: 8, z: 8 (z_hi: 2, z_lo: 4; z = z_hi * 4 + z_lo), core: 2. Of those that a mesh axis runs over, the one named last changes fastest.
Arguments:
- queries: bfloat16 [16384, 2048], P('blk', 'col'), may hold values from -1200 to 1200
- keys: bfloat16 [16384, 512], P(('blk', 'col')), may hold values from -4 to 4
- values: bfloat16 [16384, 512], P(('blk', 'col')), may hold values from -6 to 6
- positions: int32 [16384], P('blk'), may hold values from 0 to 16383, as said below
Outputs:
- attended: float32 [16384, 2048], P('blk', 'col')
- log_norm: float32 [16384, 16], P('blk', 'col')
Inputs may be any that keep to these rules, and one draw needn't show every extreme that they name: A permutation of 0 to 16383 made of runs of 128 consecutive positions, each run stored ascending in 128 consecutive rows that start at a multiple of 128.
All inputs are finite; a program needn't handle non-finite values.
Results may differ from a plain program's by a relative error of at most 0.0034.
Values may be sent and summed in bfloat16 or wider, within the bound.
No kernel may reach another device: no remote copies, remote signals or barrier semaphores. Data moves between devices by JAX's collectives and lax.ppermute only.
A program may use at most 64 MiB of HBM per device.

v0:
```python
import math

import jax
import jax.numpy as jnp
from jax import lax
from jax.sharding import PartitionSpec as P

HQ = 16
HK = 4
DH = 128


def swapped(value, axis, distance):
    mask = 2**distance
    pairs = [(source, source ^ mask) for source in range(lax.axis_size(axis))]
    return lax.ppermute(value, axis, pairs)


def side_by_side(arrays, axis, split_dim, concat_dim, along):
    ends, at = ([], 0)
    for a in arrays[:-1]:
        at += a.shape[along]
        ends.append(at)
    both = jnp.concatenate(arrays, axis=along)
    return tuple(
        jnp.split(
            lax.all_to_all(both, axis, split_axis=split_dim, concat_axis=concat_dim, tiled=True),
            ends,
            axis=along,
        )
    )


def sent_together(arrays, axis, dim, along):
    ends, at = ([], 0)
    for a in arrays[:-1]:
        at += a.shape[along]
        ends.append(at)
    both = jnp.concatenate(arrays, axis=along)
    return tuple(jnp.split(lax.all_gather(both, axis, axis=dim, tiled=True), ends, axis=along))


def spread_heads(array, groups):
    count = array.shape[0]
    heads = array.reshape(count, HK, DH)
    return jnp.repeat(heads, groups // HK, axis=1)


def body(queries, keys, values, positions):
    ncol = lax.axis_size("col")
    column = lax.axis_index("col")
    rows = queries.shape[0]
    share = keys.shape[0]
    groups = ncol // 2
    heads_here = HQ // groups
    kv_slots = max(1, HK // groups)
    ratio = heads_here // kv_slots
    own = HQ // ncol
    scale = 1.0 / math.sqrt(DH)
    side = column % 2
    partner = swapped(queries, "col", 0)
    q_rows = jnp.where(
        side == 0,
        jnp.concatenate([queries, partner], axis=1),
        jnp.concatenate([partner, queries], axis=1),
    )
    half = share // 2
    width = kv_slots * DH
    k_parts = (
        spread_heads(keys, groups)
        .reshape(2, half, groups, width)
        .transpose(2, 0, 1, 3)
        .reshape(ncol, half, width)
    )
    v_parts = (
        spread_heads(values, groups)
        .reshape(2, half, groups, width)
        .transpose(2, 0, 1, 3)
        .reshape(ncol, half, width)
    )
    k_rows, v_rows = side_by_side((k_parts, v_parts), "col", 0, 1, 2)
    k_rows = k_rows[0]
    v_rows = v_rows[0]
    k_pos = lax.dynamic_index_in_dim(
        positions.reshape(ncol, 2, half), side, 1, keepdims=False
    ).reshape(ncol * half)
    q_split = q_rows.reshape(rows, kv_slots, ratio, DH)
    start_state = (
        jnp.full((heads_here, rows), -1e30, jnp.float32),
        jnp.zeros((heads_here, rows), jnp.float32),
        jnp.zeros((heads_here, rows, DH), jnp.float32),
    )
    carry = start_state
    key_piece, value_piece, pos_piece = (
        *sent_together((k_rows, v_rows), "blk", 0, 1),
        lax.all_gather(k_pos, "blk", axis=0, tiled=True),
    )
    length = key_piece.shape[0]
    block = math.gcd(length, 128)

    def attend(state, span):
        running, totals, sums = state
        key_block, value_block, pos_block = span
        scores = jnp.einsum(
            "rsgd,ksd->sgrk",
            q_split,
            key_block.reshape(block, kv_slots, DH),
            preferred_element_type=jnp.float32,
        )
        scores = scores.reshape(heads_here, rows, block) * scale
        visible = pos_block[None, :] <= positions[:, None]
        highest = jnp.max(jnp.where(visible, scores, -1e30), axis=-1)
        updated = jnp.maximum(running, highest)
        weights = jnp.where(visible, jnp.exp(scores - updated[..., None]), 0.0)
        factor = jnp.exp(running - updated)
        totals = totals * factor + jnp.sum(weights, axis=-1)
        rounded = weights.astype(jnp.bfloat16).reshape(kv_slots, ratio, rows, block)
        mixed = jnp.einsum(
            "sgrk,ksd->sgrd",
            rounded,
            value_block.reshape(block, kv_slots, DH),
            preferred_element_type=jnp.float32,
        )
        sums = sums * factor[..., None] + mixed.reshape(heads_here, rows, DH)
        return (updated, totals, sums)

    def visit(state, span):
        return (attend(state, span), None)

    spans = (
        key_piece.reshape(length // block, block, key_piece.shape[1]),
        value_piece.reshape(length // block, block, value_piece.shape[1]),
        pos_piece.reshape(length // block, block),
    )
    carry, unused = lax.scan(visit, carry, spans)
    running, totals, sums = carry
    mine = [lax.dynamic_slice_in_dim(x, side * own, own, 0) for x in (running, totals, sums)]
    theirs = [
        lax.dynamic_slice_in_dim(x, (1 - side) * own, own, 0) for x in (running, totals, sums)
    ]
    other_max, other_total, other_sum = swapped((theirs[0], theirs[1], theirs[2]), "col", 0)
    merged_max = jnp.maximum(mine[0], other_max)
    first = jnp.exp(mine[0] - merged_max)
    second = jnp.exp(other_max - merged_max)
    totals = mine[1] * first + other_total * second
    sums = mine[2] * first[..., None] + other_sum * second[..., None]
    running = merged_max
    output_heads = sums / totals[..., None]
    lognorm = running + jnp.log(totals)
    attended = output_heads.transpose(1, 0, 2).reshape(rows, own * DH)
    return (attended, lognorm.T)


def solution(mesh):
    placed = (P("blk", "col"), P(("blk", "col"), None), P(("blk", "col"), None), P("blk"))
    return jax.shard_map(
        body,
        mesh=mesh,
        in_specs=placed,
        out_specs=(P("blk", "col"), P("blk", "col")),
        check_vma=False,
    )
```

profile of v0, /device:TPU:6, one launch (start us, length us, event | category | flops | bytes accessed | tf_op | source)
XLA Modules:
  0.0 272.9 jit_solution(1717646847360626863)
XLA Ops:
  8.8 16.4 %all_to_all.12 = bf16[16,16,256]{2,1,0:T(8,128)(2,1)S(1)} all-to-all(bf16[16,16,256]{2,1,0:T(8,128)(2,1)S(1)} %pad_maximum_fusion), channel_id=1, replica_groups=mesh['blk'=32,'col'=16] {'col'}, dimensions={0} | all-to-all | bytes 262144 | tf_op jit(solution)/shard_map/all_to_all | solution.py:27
  26.9 2.4 collective-permute-start
  30.3 55.4 %all-gather = s32[32,1,256]{2,1,0:T(1,128)S(1)} all-gather(s32[1,1,256]{2,1,0:T(1,128)S(1)} %reshape.106), channel_id=1, replica_groups=mesh['blk'=32,'col'=16] {'blk'}, dimensions={0}, use_global_device_ids=true | all-gather | bytes 33792 | tf_op jit(solution)/shard_map/all_gather | solution.py:96
  85.9 49.2 %all-gather.3.cloned.1.call-done = bf16[8192,256]{1,0:T(8,128)(2,1)} async-done(((bf16[256,256]{1,0:T(8,128)(2,1)}), bf16[8192,256]{1,0:T(8,128)(2,1)}) %all-gather.3.cloned.1.call-update) | async-done | bytes 4194320 | tf_op jit(solution)/shard_map/all_gather | solution.py:40
  135.0 3.8 %fusion.24 = (bf16[8192,128]{1,0:T(8,128)(2,1)S(1)}, bf16[8192,128]{1,0:T(8,128)(2,1)}) fusion(bf16[8192,256]{1,0:T(8,128)(2,1)} %all-gather.3.cloned.1.call-done), kind=kLoop, calls=%fused_computation.51 | loop fusion | bytes 8388608 | tf_op jit(solution)/shard_map/split | solution.py:40
  138.9 114.2 %while.15 = (s32[]{:T(128)}, f32[2,512]{1,0:T(2,128)S(1)}, f32[2,512]{1,0:T(2,128)S(1)}, f32[2,512,128]{2,1,0:T(8,128)S(1)}, s32[64,128]{1,0:T(8,128)S(1)}, /*in...) while((s32[]{:T(128)}, f32[2,512]{1,0:T(2,128)S(1)}, ...), condition=%wide.region_3.4_spmd.clone, body=%wide.region_0.3_spmd.clone.sunk | while | flops 68752384 | bytes 3280525 | solution.py:135
  139.0 1.0 fusion.37
  140.8 1.0 fusion.37
  142.5 1.0 fusion.37
  147.9 1.0 fusion.37
  149.7 1.0 fusion.37
  160.4 1.0 fusion.37
  162.2 1.0 fusion.37
  171.1 1.0 fusion.37
  172.9 1.0 fusion.37
  181.8 1.0 fusion.37
  183.6 1.0 fusion.37
  194.3 1.0 fusion.37
  196.1 1.0 fusion.37
  205.0 1.0 fusion.37
  253.2 2.2 collective-permute-start.2
  255.4 3.6 %collective-permute-start.3 = (f32[1,512]{1,0:T(1,128)S(1)}, f32[1,512]{1,0:T(1,128)S(1)}, u32[]{:S(2)}, u32[]{:S(2)}) collective-permute-start(f32[1,512]{1,0:T(1,128)S(1)} %constant_dynamic-slice_fusion.1), channel_id=1, source_target_pairs={{0,1},{1,0},{2,3},{3,2},{4,5},{5,4},{6,7},{7,6},{8,9},{9,8},{10,11... | collective-permute-start | bytes 6152 | tf_op jit(solution)/shard_map/ppermute | solution.py:16
  259.0 2.2 collective-permute-start.1
  261.2 2.3 collective-permute-done.3
  (528 shorter events, 103.1 us)
Async XLA Ops:
  7.2 0.8 copy-start
  7.2 127.9 %all-gather.3.cloned.1.call-start = ((), (), s32[]{:S(2)}) async-start(), calls=%async_computation.1 | async-start | bytes 4325376 | tf_op jit(solution)/shard_map/all_gather | solution.py:40
  26.9 58.7 %collective-permute-start = (bf16[512,128]{0,1:T(8,128)(2,1)S(1)}, bf16[512,128]{0,1:T(8,128)(2,1)S(1)}, u32[]{:S(2)}, u32[]{:S(2)}) collective-permute-start(bf16[512,128]{0,1:T(8,128)(2,1)S(1)} %copy.20), channel_id=1, source_target_pairs={{0,1},{1,0},{2,3},{3,2},{4,5},{5,4},{6,7},{7,6},{8,9},{9,8},{10,11... | collective-permute-start | bytes 393224 | tf_op jit(solution)/shard_map/ppermute | solution.py:16
  85.9 53.0 %copy-start.1 = (s32[512]{0:T(512)S(1)}, s32[512]{0:T(512)}, u32[]{:S(2)}) copy-start(s32[512]{0:T(512)} %param.9) | copy-start | bytes 6148
  253.2 12.0 %collective-permute-start.2 = (f32[1,512,128]{2,1,0:T(8,128)S(1)}, f32[1,512,128]{2,1,0:T(8,128)S(1)}, u32[]{:S(2)}, u32[]{:S(2)}) collective-permute-start(f32[1,512,128]{2,1,0:T(8,128)S(1)} %constant_dynamic-slice_fusion.2), channel_id=1, source_target_pairs={{0,1},{1,0},{2,3},{3,2},{4,5},{5,4},{6,7},{7,6},{8,9},{9,8},{10,11... | collective-permute-start | bytes 786440 | tf_op jit(solution)/shard_map/ppermute | solution.py:16
  255.4 8.2 %collective-permute-start.3 = (f32[1,512]{1,0:T(1,128)S(1)}, f32[1,512]{1,0:T(1,128)S(1)}, u32[]{:S(2)}, u32[]{:S(2)}) collective-permute-start(f32[1,512]{1,0:T(1,128)S(1)} %constant_dynamic-slice_fusion.1), channel_id=1, source_target_pairs={{0,1},{1,0},{2,3},{3,2},{4,5},{5,4},{6,7},{7,6},{8,9},{9,8},{10,11... | collective-permute-start | bytes 6152 | tf_op jit(solution)/shard_map/ppermute | solution.py:16
  259.0 5.5 %collective-permute-start.1 = (f32[1,512]{1,0:T(1,128)S(1)}, f32[1,512]{1,0:T(1,128)S(1)}, u32[]{:S(2)}, u32[]{:S(2)}) collective-permute-start(f32[1,512]{1,0:T(1,128)S(1)} %constant_dynamic-slice_fusion.3), channel_id=1, source_target_pairs={{0,1},{1,0},{2,3},{3,2},{4,5},{5,4},{6,7},{7,6},{8,9},{9,8},{10,11... | collective-permute-start | bytes 6152 | tf_op jit(solution)/shard_map/ppermute | solution.py:16
Sparse Core Ops, SparseCore 0:
  26.0 108.9 all-gather.2
where the time goes:
time: 278 us; the launch traced here: 273 us
  matrix products  93 us (33%)
  blocking collectives  71.8 us (26%)
  waiting for transfers between devices  52.5 us (19%)
  other arithmetic  18.8 us (7%)
  between operations  14.2 us (5%)
  starting transfers between devices  10.5 us (4%)
  local copies, waits for them, and re-layouts  8.2 us (3%)
  loops' own time  3.99 us (1%)
    dot_general x64, matrix products, attend(): jnp.einsum('rsgd,ksd->sgrk', q_split, key_block.reshape(block, kv_slots,...  64.7 us
    all_gather x1, blocking collectives, body(): lax.all_gather(k_pos, 'blk', axis=0, tiled=True)  55.4 us
    all_gather x1, waiting for transfers between devices, sent_together(): lax.all_gather(both, axis, axis=dim, tiled=True)  49.2 us
    dot_general x64, matrix products, attend(): jnp.einsum('sgrk,ksd->sgrd', rounded, value_block.reshape(block, kv_slots...  28.3 us
    all_to_all x1, blocking collectives, side_by_side(): lax.all_to_all(both, axis, split_axis=split_dim, concat_axis=concat_dim,...  16.4 us
    ppermute x4, starting transfers between devices, swapped(): return lax.ppermute(value, axis, pairs)  10.4 us
    reduce_sum x64, other arithmetic, attend(): totals = totals * factor + jnp.sum(weights, axis=-1)  8.12 us
    le x64, other arithmetic, attend(): visible = pos_block[None, :] <= positions[:, None]  6.67 us
  transfers between devices with their start and end apart: 5, of which 3 were waited for; matrix products, arithmetic and copies ran while one was open for 1% of the time, Pallas kernels for 0%

commit v1 on v0

v1 whole, which is shorter than its diff:
```python
import math

import jax
import jax.numpy as jnp
from jax import lax
from jax.experimental import pallas as pl
from jax.experimental.pallas import tpu as pltpu
from jax.sharding import PartitionSpec as P

HQ = 16
HK = 4
DH = 128
STRIPE = 128
NY, NZH, NC, NX, NZL = 8, 2, 2, 4, 4
SUB = 64
NST = 8
BK = NST * SUB
ROWS = 2 * BK + 16
NQ = 8
C2 = math.log2(math.e) / math.sqrt(DH)
LN2 = math.log(2.0)
MASKED = -1e30
EMPTY = -1e29
VM = pltpu.VMEM
SM = pltpu.SMEM


def flat_groups(key):
    found = {}
    for b in range(NY * NZH * NC):
        for c in range(NX * NZL):
            k = key(b // 4, (b // 2) % 2, b % 2, c // 4, c % 4)
            found.setdefault(k, []).append(b * NX * NZL + c)
    return list(found.values())


KV_GROUPS = flat_groups(lambda y, zh, c, x, zl: (y, c, zl % 2))
OUT_GROUPS = flat_groups(lambda y, zh, c, x, zl: (y, zh, x, zl // 2))


def pairs(move):
    out = []
    for b in range(NY * NZH * NC):
        for c in range(NX * NZL):
            y, zh, co, x, zl = move(b // 4, (b // 2) % 2, b % 2, c // 4, c % 4)
            out.append((b * 16 + c, ((y % NY) * 4 + zh * 2 + co) * 16 + x * 4 + zl))
    return out


UP = pairs(lambda y, zh, c, x, zl: (y + 1, zh, c, x, zl))
DOWN = pairs(lambda y, zh, c, x, zl: (y - 1, zh, c, x, zl))
LAST = pairs(lambda y, zh, c, x, zl: (y + 1 - 2 * c, zh, c, x, zl))
CORE = pairs(lambda y, zh, c, x, zl: (y, zh, 1 - c, x, zl))
ZPAIR = pairs(lambda y, zh, c, x, zl: (y, zh, c, x, zl ^ 1))
DIAG = pairs(lambda y, zh, c, x, zl: (y, zh, 1 - c, x, zl ^ 1))


def send(value, perm):
    return lax.ppermute(value, ("blk", "col"), perm)


def call(kernel, out, in_spaces, scratch=(), alias=None, name=None, flops=0):
    vm = pl.BlockSpec(memory_space=VM)
    sm = pl.BlockSpec(memory_space=SM)
    return pl.pallas_call(
        kernel,
        out_shape=out,
        in_specs=[sm if s == "s" else vm for s in in_spaces],
        out_specs=jax.tree.map(lambda _: vm, out),
        scratch_shapes=list(scratch),
        input_output_aliases=alias or {},
        name=name,
        cost_estimate=pl.CostEstimate(flops=flops, transcendentals=0, bytes_accessed=0) if flops else None,
        compiler_params=pltpu.CompilerParams(vmem_limit_bytes=40 * 1024 * 1024),
    )


def pack_kernel(pos_ref, k_ref, v_ref, o_ref):
    tile = jnp.full((16, DH), pos_ref[0].astype(jnp.float32), jnp.float32).astype(jnp.bfloat16)
    for m in range(16):
        x = (m // 2) % 4
        o_ref[m, 0:32, :] = k_ref[:, x * DH : (x + 1) * DH]
        o_ref[m, 32:64, :] = v_ref[:, x * DH : (x + 1) * DH]
        o_ref[m, 64:80, :] = tile


def scalar_of(row):
    return jnp.max(row.astype(jnp.float32)).astype(jnp.int32)


def prep_kernel(r_ref, o_ref, v_scr, p_scr):
    pos = []
    for j in range(NST):
        m = (j // 4) * 8 + (j % 4) * 2
        pos.append(scalar_of(r_ref[m, 64:65, :]))
    for j in range(NST):
        rank = jnp.int32(0)
        for i in range(NST):
            if i != j:
                rank = rank + (pos[i] < pos[j]).astype(jnp.int32)
        p_scr[rank] = pos[j]
        m = (j // 4) * 8 + (j % 4) * 2
        at = pl.multiple_of(rank * SUB, SUB)
        kk = jnp.concatenate([r_ref[m, 0:32, :], r_ref[m + 1, 0:32, :]], axis=0)
        vv = jnp.concatenate([r_ref[m, 32:64, :], r_ref[m + 1, 32:64, :]], axis=0)
        o_ref[pl.ds(at, SUB), :] = kk
        v_scr[pl.ds(at, SUB), :] = vv.astype(jnp.float32)
    for t in range(BK // DH):
        o_ref[BK + t * DH : BK + (t + 1) * DH, :] = v_scr[t * DH : (t + 1) * DH, :].T.astype(jnp.bfloat16)
    row = lax.broadcasted_iota(jnp.int32, (16, DH), 0)
    tile = jnp.zeros((16, DH), jnp.float32)
    for r in range(NST):
        tile = jnp.where(row == r, p_scr[r].astype(jnp.float32), tile)
    o_ref[2 * BK : ROWS, :] = tile.astype(jnp.bfloat16)


def qext_kernel(pos_ref, q_ref, o_ref):
    o_ref[0:512, :] = q_ref[...]
    row = lax.broadcasted_iota(jnp.int32, (16, DH), 0)
    tile = jnp.zeros((16, DH), jnp.float32)
    for r in range(4):
        tile = jnp.where(row == r, pos_ref[r].astype(jnp.float32), tile)
    o_ref[512:528, :] = tile.astype(jnp.bfloat16)


def attend_kernel(nblocks, first, side_ref, qo_ref, qz_ref, qc_ref, qd_ref, *rest):
    blocks = rest[:nblocks]
    if first:
        acc_ref, m_ref, q_ref, off_ref, qp, qt, kp = rest[nblocks:]
        accin_ref = min_ref = None
    else:
        accin_ref, min_ref, acc_ref, m_ref, q_ref, off_ref, qp, qt, kp = rest[nblocks:]
    side = side_ref[0]
    pos = []
    for t in range(4):
        q_ref[t, 0:128, :] = qo_ref[t * 128 : (t + 1) * 128, :]
        q_ref[t, 128:256, :] = qz_ref[t * 128 : (t + 1) * 128, :]
        q_ref[4 + t, 0:128, :] = qc_ref[t * 128 : (t + 1) * 128, :]
        q_ref[4 + t, 128:256, :] = qd_ref[t * 128 : (t + 1) * 128, :]
    for ref in (qo_ref, qc_ref):
        for t in range(4):
            pos.append(scalar_of(ref[512 + t : 513 + t, :]))
    for j in range(NQ):
        rank = jnp.int32(0)
        for i in range(NQ):
            if i != j:
                rank = rank + (pos[i] < pos[j]).astype(jnp.int32)
        qp[rank] = pos[j]
        qt[rank] = jnp.int32(j)
    for n, blk in enumerate(blocks):
        for j in range(NST):
            kp[n * NST + j] = scalar_of(blk[2 * BK + j : 2 * BK + j + 1, :])
    r = lax.broadcasted_iota(jnp.int32, (SUB, 256), 0)
    lane = lax.broadcasted_iota(jnp.int32, (SUB, 256), 1)
    off_ref[...] = (r // 32) * 64 + side * 32 + r % 32 - lane % 128
    ones = jnp.ones((16, BK), jnp.bfloat16)
    if first:
        acc_ref[...] = jnp.zeros_like(acc_ref)
        m_ref[...] = jnp.full(m_ref.shape, EMPTY, jnp.float32)
    else:
        acc_ref[...] = accin_ref[...]
        m_ref[...] = min_ref[...]

    def local(qpos, t, keys):
        scores = []
        for n, blk in enumerate(blocks):
            s = lax.dot_general(
                blk[0:keys, :], q_ref[t], (((1,), (1,)), ((), ())), preferred_element_type=jnp.float32
            )
            parts = []
            for j in range(keys // SUB):
                gap = (qpos - kp[n * NST + j]) * STRIPE
                parts.append(jnp.where(off_ref[...] <= gap, s[j * SUB : (j + 1) * SUB, :] * C2, MASKED))
            scores.append(jnp.concatenate(parts, axis=0))
        top = jnp.max(scores[0], axis=0, keepdims=True)
        for s in scores[1:]:
            top = jnp.maximum(top, jnp.max(s, axis=0, keepdims=True))
        mixed = None
        for s, blk in zip(scores, blocks):
            p = jnp.exp2(s - top).astype(jnp.bfloat16)
            vt = jnp.concatenate(
                [blk[BK + i * DH : BK + (i + 1) * DH, :] for i in range(keys // DH)], axis=1
            )
            vt = jnp.concatenate([vt, ones[:, 0:keys]], axis=0)
            part = jnp.dot(vt, p, preferred_element_type=jnp.float32)
            mixed = part if mixed is None else mixed + part
        return top, mixed

    def two(i, keys):
        found = [(qt[2 * i + k],) + local(qp[2 * i + k], qt[2 * i + k], keys) for k in range(2)]
        for t, top, mixed in found:
            old = m_ref[t, 0:1, :]
            new = jnp.maximum(old, top)
            acc_ref[t] = acc_ref[t] * jnp.exp2(old - new) + mixed * jnp.exp2(top - new)
            m_ref[t] = jnp.broadcast_to(new, (8, 256))

    def pair(i, carry):
        far = qp[2 * i + 1]
        wide = kp[NST // 2] <= far
        seen = kp[0] <= far
        for n in range(1, nblocks):
            wide = jnp.logical_or(wide, kp[n * NST + NST // 2] <= far)
            seen = jnp.logical_or(seen, kp[n * NST] <= far)

        @pl.when(wide)
        def _():
            two(i, BK)

        @pl.when(jnp.logical_and(seen, jnp.logical_not(wide)))
        def _():
            two(i, BK // 2)

        return carry

    lax.fori_loop(0, NQ // 2, pair, 0)


def partial_kernel(who_ref, acc_ref, m_ref, o_ref):
    core, side = who_ref[0], who_ref[1]
    for dc in range(2):
        for dz in range(2):
            member = (core + dc - 2 * core * dc) * 2 + (side + dz - 2 * side * dz)
            rows = []
            for t in range(4):
                st = dc * 4 + t
                lanes = slice(dz * 128, dz * 128 + 128)
                total = acc_ref[st, 128:129, lanes]
                top = m_ref[st, 0:1, lanes]
                seen = total > 0.0
                inv = jnp.where(seen, 1.0 / jnp.where(seen, total, 1.0), 0.0)
                o_ref[member, t * 128 : (t + 1) * 128, :] = (acc_ref[st, 0:128, lanes] * inv).T.astype(jnp.bfloat16)
                rows.append(jnp.where(seen, top + jnp.log2(jnp.where(seen, total, 1.0)), EMPTY))
            lse = jnp.concatenate(rows, axis=0)
            hi = lse.astype(jnp.bfloat16).astype(jnp.float32)
            mid = (lse - hi).astype(jnp.bfloat16).astype(jnp.float32)
            low = lse - hi - mid
            o_ref[member, 512:528, :] = jnp.concatenate(
                [hi, mid, low, jnp.zeros((4, 128), jnp.float32)], axis=0
            ).astype(jnp.bfloat16)


def merge_kernel(i_ref, o_ref, l_ref):
    lses = []
    for m in range(4):
        tile = i_ref[m, 512:528, :].astype(jnp.float32)
        lses.append(tile[0:4] + tile[4:8] + tile[8:12])
    top = jnp.maximum(jnp.maximum(lses[0], lses[1]), jnp.maximum(lses[2], lses[3]))
    ws = [jnp.exp2(x - top) for x in lses]
    total = ws[0] + ws[1] + ws[2] + ws[3]
    l_ref[...] = (top + jnp.log2(total)) * LN2
    inv = 1.0 / total
    for t in range(4):
        out = None
        for m in range(4):
            w = jnp.broadcast_to((ws[m] * inv)[t : t + 1, :], (128, 128)).T
            part = i_ref[m, t * 128 : (t + 1) * 128, :].astype(jnp.float32) * w
            out = part if out is None else out + part
        o_ref[t * 128 : (t + 1) * 128, :] = out


def body(queries, keys, values, positions):
    bf, f32 = jnp.bfloat16, jnp.float32
    blk, col = lax.axis_index("blk"), lax.axis_index("col")
    core, side, x = blk % 2, col % 2, col // 4
    stripes = positions.reshape(4, STRIPE)[:, 0] // STRIPE
    mine = lax.dynamic_slice_in_dim(stripes, x, 1)
    who = jnp.stack([core, side]).astype(jnp.int32)
    side_arr = side.reshape(1).astype(jnp.int32)

    packed = call(pack_kernel, jax.ShapeDtypeStruct((16, 80, DH), bf), "svv", name="pack")(mine, keys, values)
    got = lax.all_to_all(packed, ("blk", "col"), 0, 0, axis_index_groups=KV_GROUPS, tiled=False)
    own = call(
        prep_kernel,
        jax.ShapeDtypeStruct((ROWS, DH), bf),
        "v",
        scratch=[VM((BK, DH), f32), SM((NST,), jnp.int32)],
        name="prep",
    )(got)
    qo = call(qext_kernel, jax.ShapeDtypeStruct((528, DH), bf), "sv", name="qext")(stripes, queries)

    up, down = [send(own, UP)], [send(own, DOWN)]
    qc, qz, qd = send(qo, CORE), send(qo, ZPAIR), send(qo, DIAG)
    qs = (side_arr, qo, qz, qc, qd)
    for step in range(2):
        up.append(send(up[-1], UP))
        down.append(send(down[-1], DOWN))
    last = send(jnp.where(core == 0, up[2], down[2]), LAST)

    state = (jax.ShapeDtypeStruct((NQ, 144, 256), f32), jax.ShapeDtypeStruct((NQ, 8, 256), f32))

    def attend(blocks, carry):
        n = len(blocks)
        first = carry is None
        kernel = lambda *refs: attend_kernel(n, first, *refs)
        scratch = [
            VM((NQ, 256, DH), bf),
            VM((SUB, 256), jnp.int32),
            SM((NQ,), jnp.int32),
            SM((NQ,), jnp.int32),
            SM((2 * NST,), jnp.int32),
        ]
        args = qs + tuple(blocks) + (() if first else carry)
        return call(
            kernel,
            state,
            "svvvv" + "v" * (n + (0 if first else 2)),
            scratch=scratch,
            alias=None if first else {5 + n: 0, 6 + n: 1},
            flops=n * 2_000_000_000,
            name=f"attend{n}",
        )(*args)

    carry = attend([own], None)
    for a, b in zip(up, down):
        carry = attend([a, b], carry)
    carry = attend([last], carry)
    part = call(partial_kernel, jax.ShapeDtypeStruct((4, 528, DH), bf), "svv", name="partial")(who, *carry)
    parts = lax.all_to_all(part, ("blk", "col"), 0, 0, axis_index_groups=OUT_GROUPS, tiled=False)
    attended, lognorm = call(
        merge_kernel,
        (jax.ShapeDtypeStruct((512, DH), f32), jax.ShapeDtypeStruct((4, 128), f32)),
        "v",
        name="merge",
    )(parts)
    return attended, lognorm.reshape(512, 1)


def solution(mesh):
    placed = (P("blk", "col"), P(("blk", "col"), None), P(("blk", "col"), None), P("blk"))
    return jax.shard_map(
        body,
        mesh=mesh,
        in_specs=placed,
        out_specs=(P("blk", "col"), P("blk", "col")),
        check_vma=False,
    )
```

time: 278 us -> 96.8 us (0.35)
  the two profiles are of different devices: /device:TPU:6 before, /device:TPU:1 now
where the time goes in v1:
time: 96.8 us; the launch traced here: 96.9 us
  starting transfers between devices  45.8 us (47%)
  Pallas kernels  22.9 us (24%)
  blocking collectives  19.9 us (21%)
  waiting for transfers between devices  4.38 us (5%)
  local copies, waits for them, and re-layouts  2.94 us (3%)
    ppermute x10, starting transfers between devices, send(): return lax.ppermute(value, ('blk', 'col'), perm)  32.4 us
    all_to_all x1, blocking collectives, body(): lax.all_to_all(part, ('blk', 'col'), 0, 0, axis_index_groups=OUT_GROUPS,...  19.9 us
    pallas_call x5, Pallas kernels, attend(): call(kernel, state, 'svvvv' + 'v' * (n + (0 if first else 2)), scratch=sc...  18.8 us
    all_to_all x1, starting transfers between devices, body(): lax.all_to_all(packed, ('blk', 'col'), 0, 0, axis_index_groups=KV_GROUPS,...  13.4 us
    all_to_all x1, waiting for transfers between devices, body(): lax.all_to_all(packed, ('blk', 'col'), 0, 0, axis_index_groups=KV_GROUPS,...  4.35 us
  transfers between devices with their start and end apart: 11, of which 1 were waited for; matrix products, arithmetic and copies ran while one was open for 0% of the time, Pallas kernels for 17%

profile of v1, /device:TPU:1, one launch (start us, length us, event | category | flops | bytes accessed | tf_op | source)
XLA Modules:
  0.0 96.9 jit_solution(12643729207178910123)
XLA Ops:
  0.7 0.8 slice_reduce_fusion
  2.1 0.8 copy-done.1
  2.9 0.8 copy-done.2
  3.6 1.4 %pack.1 = bf16[16,80,128]{2,1,0:T(8,128)(2,1)} custom-call(s32[1]{0:T(128)} %dynamic_slice.3.pos_ref, bf16[32,512]{1,0:T(8,128)(2,1)S(1)} %copy-done.1, bf16[32,512]{1,0:T(8,128)(2,1)S(1)} %copy-done.2), custom_call_target="tpu_custom_call" | custom-call | tf_op jit(solution)/shard_map/pack/pallas_call | solution.py:270
  5.0 13.4 %all-to-all-start = ((bf16[16,80,128]{2,1,0:T(8,128)(2,1)}), bf16[16,80,128]{2,1,0:T(8,128)(2,1)S(1)}, u32[]{:S(2)}, u32[]{:S(2)}) async-start(bf16[16,80,128]{2,1,0:T(8,128)(2,1)} %pack.1), calls=%async_computation | async-start | bytes 655360 | tf_op jit(solution)/shard_map/all_to_all | solution.py:271
  19.0 3.1 %collective-permute-start = (bf16[528,128]{1,0:T(8,128)(2,1)S(1)}, bf16[528,128]{1,0:T(8,128)(2,1)S(1)}, u32[]{:S(2)}, u32[]{:S(2)}) collective-permute-start(bf16[528,128]{1,0:T(8,128)(2,1)S(1)} %qext.1.refs_1_), channel_id=1, source_target_pairs={{0,1},{1,0},{2,3},{3,2},{4,5},{5,4},{6,7},{7,6},{8,9},{9,8},{10,11... | collective-permute-start | bytes 405512 | tf_op jit(solution)/shard_map/ppermute | solution.py:59
  22.1 3.1 %collective-permute-start.1 = (bf16[528,128]{1,0:T(8,128)(2,1)S(1)}, bf16[528,128]{1,0:T(8,128)(2,1)S(1)}, u32[]{:S(2)}, u32[]{:S(2)}) collective-permute-start(bf16[528,128]{1,0:T(8,128)(2,1)S(1)} %qext.1.refs_1_), channel_id=1, source_target_pairs={{0,16},{1,17},{2,18},{3,19},{4,20},{5,21},{6,22},{7,23},{8,24},{9,... | collective-permute-start | bytes 405512 | tf_op jit(solution)/shard_map/ppermute | solution.py:59
  25.3 2.1 %collective-permute-start.2 = (bf16[528,128]{1,0:T(8,128)(2,1)S(1)}, bf16[528,128]{1,0:T(8,128)(2,1)S(1)}, u32[]{:S(2)}, u32[]{:S(2)}) collective-permute-start(bf16[528,128]{1,0:T(8,128)(2,1)S(1)} %qext.1.refs_1_), channel_id=1, source_target_pairs={{0,17},{1,16},{2,19},{3,18},{4,21},{5,20},{6,23},{7,22},{8,25},{9,... | collective-permute-start | bytes 405512 | tf_op jit(solution)/shard_map/ppermute | solution.py:59
  27.4 4.4 %all-to-all-done.r_ref = bf16[16,80,128]{2,1,0:T(8,128)(2,1)S(1)} async-done(((bf16[16,80,128]{2,1,0:T(8,128)(2,1)}), bf16[16,80,128]{2,1,0:T(8,128)(2,1)S(1)}, u32[]{:S(2)}, u32[]{:S(2)}) %all-to-all-start) | async-done | bytes 327712 | tf_op jit(solution)/shard_map/all_to_all | solution.py:271
  32.0 3.2 %collective-permute-start.3 = (bf16[1040,128]{1,0:T(8,128)(2,1)S(1)}, bf16[1040,128]{1,0:T(8,128)(2,1)S(1)}, u32[]{:S(2)}, u32[]{:S(2)}) collective-permute-start(bf16[1040,128]{1,0:T(8,128)(2,1)S(1)} %prep.1.refs_5_), channel_id=1, source_target_pairs={{0,64},{1,65},{2,66},{3,67},{4,68},{5,69},{6,70},{7,71},{8,72},{9,... | collective-permute-start | bytes 798728 | tf_op jit(solution)/shard_map/ppermute | solution.py:59
  35.3 3.8 %collective-permute-start.6 = (bf16[1040,128]{1,0:T(8,128)(2,1)S(1)}, bf16[1040,128]{1,0:T(8,128)(2,1)S(1)}, u32[]{:S(2)}, u32[]{:S(2)}) collective-permute-start(bf16[1040,128]{1,0:T(8,128)(2,1)S(1)} %prep.1.refs_5_), channel_id=1, source_target_pairs={{0,448},{1,449},{2,450},{3,451},{4,452},{5,453},{6,454},{7,455},{8... | collective-permute-start | bytes 798728 | tf_op jit(solution)/shard_map/ppermute | solution.py:59
  39.2 3.0 %attend1.2 = (f32[8,144,256]{2,1,0:T(8,128)S(1)}, f32[8,8,256]{2,1,0:T(8,128)S(1)}) custom-call(s32[1]{0:T(128)} %bitcast.1.refs_0_, bf16[528,128]{1,0:T(8,128)(2,1)S(1)} %qext.1.refs_1_, bf16[528,128]{1,0:T(8,128)(2,1)S(1)} %collective-permute-done.refs_2_, bf16[528,128]{1,0:T(8,128)(2,1)S(1)} %collective-permute-done.1.refs_3_, ...), custom_call_target="tpu_custom_call" | custom-call | flops 2000000000 | tf_op jit(solution)/shard_map/attend1/pallas_call | solution.py:303
  42.2 2.4 %collective-permute-start.4 = (bf16[1040,128]{1,0:T(8,128)(2,1)S(1)}, bf16[1040,128]{1,0:T(8,128)(2,1)S(1)}, u32[]{:S(2)}, u32[]{:S(2)}) collective-permute-start(bf16[1040,128]{1,0:T(8,128)(2,1)S(1)} %collective-permute-done.3.refs_5_), channel_id=1, source_target_pairs={{0,64},{1,65},{2,66},{3,67},{4,68},{5,69},{6,70},{7,71},{8,72},{9,... | collective-permute-start | bytes 798728 | tf_op jit(solution)/shard_map/ppermute | solution.py:59
  44.6 4.0 %collective-permute-start.7 = (bf16[1040,128]{1,0:T(8,128)(2,1)S(1)}, bf16[1040,128]{1,0:T(8,128)(2,1)S(1)}, u32[]{:S(2)}, u32[]{:S(2)}) collective-permute-start(bf16[1040,128]{1,0:T(8,128)(2,1)S(1)} %collective-permute-done.6.refs_6_), channel_id=1, source_target_pairs={{0,448},{1,449},{2,450},{3,451},{4,452},{5,453},{6,454},{7,455},{8... | collective-permute-start | bytes 798728 | tf_op jit(solution)/shard_map/ppermute | solution.py:59
  48.7 3.9 %attend2.3 = (f32[8,144,256]{2,1,0:T(8,128)S(1)}, f32[8,8,256]{2,1,0:T(8,128)S(1)}) custom-call(s32[1]{0:T(128)} %bitcast.1.refs_0_, bf16[528,128]{1,0:T(8,128)(2,1)S(1)} %qext.1.refs_1_, bf16[528,128]{1,0:T(8,128)(2,1)S(1)} %collective-permute-done.refs_2_, ...), custom_call_target="tpu_custom_call", output_to_operand_aliasing={{0}: (7, {}), {1}: (8, {})} | custom-call | flops 4000000000 | tf_op jit(solution)/shard_map/attend2/pallas_call | solution.py:303
  52.6 1.9 %collective-permute-start.5 = (bf16[1040,128]{1,0:T(8,128)(2,1)S(1)}, bf16[1040,128]{1,0:T(8,128)(2,1)S(1)}, u32[]{:S(2)}, u32[]{:S(2)}) collective-permute-start(bf16[1040,128]{1,0:T(8,128)(2,1)S(1)} %collective-permute-done.4.refs_5_), channel_id=1, source_target_pairs={{0,64},{1,65},{2,66},{3,67},{4,68},{5,69},{6,70},{7,71},{8,72},{9,... | collective-permute-start | bytes 798728 | tf_op jit(solution)/shard_map/ppermute | solution.py:59
  54.5 4.6 %collective-permute-start.8 = (bf16[1040,128]{1,0:T(8,128)(2,1)S(1)}, bf16[1040,128]{1,0:T(8,128)(2,1)S(1)}, u32[]{:S(2)}, u32[]{:S(2)}) collective-permute-start(bf16[1040,128]{1,0:T(8,128)(2,1)S(1)} %collective-permute-done.7.refs_6_), channel_id=1, source_target_pairs={{0,448},{1,449},{2,450},{3,451},{4,452},{5,453},{6,454},{7,455},{8... | collective-permute-start | bytes 798728 | tf_op jit(solution)/shard_map/ppermute | solution.py:59
  59.1 4.3 %attend2.4 = (f32[8,144,256]{2,1,0:T(8,128)S(1)}, f32[8,8,256]{2,1,0:T(8,128)S(1)}) custom-call(s32[1]{0:T(128)} %bitcast.1.refs_0_, bf16[528,128]{1,0:T(8,128)(2,1)S(1)} %qext.1.refs_1_, bf16[528,128]{1,0:T(8,128)(2,1)S(1)} %collective-permute-done.refs_2_, ...), custom_call_target="tpu_custom_call", output_to_operand_aliasing={{0}: (7, {}), {1}: (8, {})} | custom-call | flops 4000000000 | tf_op jit(solution)/shard_map/attend2/pallas_call | solution.py:303
  63.5 4.1 %collective-permute-start.9 = (bf16[1040,128]{1,0:T(8,128)(2,1)S(1)}, bf16[1040,128]{1,0:T(8,128)(2,1)S(1)}, u32[]{:S(2)}, u32[]{:S(2)}) collective-permute-start(bf16[1040,128]{1,0:T(8,128)(2,1)S(1)} %broadcast_select_fusion), channel_id=1, source_target_pairs={{0,64},{1,65},{2,66},{3,67},{4,68},{5,69},{6,70},{7,71},{8,72},{9,... | collective-permute-start | bytes 798728 | tf_op jit(solution)/shard_map/ppermute | solution.py:59
  67.5 4.3 %attend2.5 = (f32[8,144,256]{2,1,0:T(8,128)S(1)}, f32[8,8,256]{2,1,0:T(8,128)S(1)}) custom-call(s32[1]{0:T(128)} %bitcast.1.refs_0_, bf16[528,128]{1,0:T(8,128)(2,1)S(1)} %qext.1.refs_1_, bf16[528,128]{1,0:T(8,128)(2,1)S(1)} %collective-permute-done.refs_2_, ...), custom_call_target="tpu_custom_call", output_to_operand_aliasing={{0}: (7, {}), {1}: (8, {})} | custom-call | flops 4000000000 | tf_op jit(solution)/shard_map/attend2/pallas_call | solution.py:303
  71.8 3.4 %attend1.3 = (f32[8,144,256]{2,1,0:T(8,128)S(1)}, f32[8,8,256]{2,1,0:T(8,128)S(1)}) custom-call(s32[1]{0:T(128)} %bitcast.1.refs_0_, bf16[528,128]{1,0:T(8,128)(2,1)S(1)} %qext.1.refs_1_, bf16[528,128]{1,0:T(8,128)(2,1)S(1)} %collective-permute-done.refs_2_, ...), custom_call_target="tpu_custom_call", output_to_operand_aliasing={{0}: (6, {}), {1}: (7, {})} | custom-call | flops 2000000000 | tf_op jit(solution)/shard_map/attend1/pallas_call | solution.py:303
  75.2 0.8 partial.1
  75.9 19.9 %all_to_all.10.i_ref = bf16[4,528,128]{2,1,0:T(8,128)(2,1)S(1)} all-to-all(bf16[4,528,128]{2,1,0:T(8,128)(2,1)S(1)} %partial.1), channel_id=1, replica_groups={{0,1,16,17},{2,3,18,19},{4,5,20,21},{6,7,22,23},{8,9,24,25},{10,11,26,2..., dimensions={0} | all-to-all | bytes 1081344 | tf_op jit(solution)/shard_map/all_to_all | solution.py:318
  95.9 1.1 %merge.1 = (f32[512,128]{1,0:T(8,128)}, f32[4,128]{1,0:T(4,128)}) custom-call(bf16[4,528,128]{2,1,0:T(8,128)(2,1)S(1)} %all_to_all.10.i_ref), custom_call_target="tpu_custom_call" | custom-call | tf_op jit(solution)/shard_map/merge/pallas_call | solution.py:319
  (20 shorter events, 1.6 us)
Async XLA Ops:
  0.6 17.8 %copy-start = (bf16[512,128]{1,0:T(8,128)(2,1)S(1)}, bf16[512,128]{1,0:T(8,128)(2,1)}, u32[]{:S(2)}) copy-start(bf16[512,128]{1,0:T(8,128)(2,1)} %q_ref.1) | copy-start | bytes 393220
  2.1 0.8 copy-start.1
  2.8 0.8 copy-start.2
  5.0 26.7 %all-to-all-start = ((bf16[16,80,128]{2,1,0:T(8,128)(2,1)}), bf16[16,80,128]{2,1,0:T(8,128)(2,1)S(1)}, u32[]{:S(2)}, u32[]{:S(2)}) async-start(bf16[16,80,128]{2,1,0:T(8,128)(2,1)} %pack.1), calls=%async_computation | async-start | bytes 655360 | tf_op jit(solution)/shard_map/all_to_all | solution.py:271
  19.0 20.2 %collective-permute-start = (bf16[528,128]{1,0:T(8,128)(2,1)S(1)}, bf16[528,128]{1,0:T(8,128)(2,1)S(1)}, u32[]{:S(2)}, u32[]{:S(2)}) collective-permute-start(bf16[528,128]{1,0:T(8,128)(2,1)S(1)} %qext.1.refs_1_), channel_id=1, source_target_pairs={{0,1},{1,0},{2,3},{3,2},{4,5},{5,4},{6,7},{7,6},{8,9},{9,8},{10,11... | collective-permute-start | bytes 405512 | tf_op jit(solution)/shard_map/ppermute | solution.py:59
  22.1 17.1 %collective-permute-start.1 = (bf16[528,128]{1,0:T(8,128)(2,1)S(1)}, bf16[528,128]{1,0:T(8,128)(2,1)S(1)}, u32[]{:S(2)}, u32[]{:S(2)}) collective-permute-start(bf16[528,128]{1,0:T(8,128)(2,1)S(1)} %qext.1.refs_1_), channel_id=1, source_target_pairs={{0,16},{1,17},{2,18},{3,19},{4,20},{5,21},{6,22},{7,23},{8,24},{9,... | collective-permute-start | bytes 405512 | tf_op jit(solution)/shard_map/ppermute | solution.py:59
  25.3 13.9 %collective-permute-start.2 = (bf16[528,128]{1,0:T(8,128)(2,1)S(1)}, bf16[528,128]{1,0:T(8,128)(2,1)S(1)}, u32[]{:S(2)}, u32[]{:S(2)}) collective-permute-start(bf16[528,128]{1,0:T(8,128)(2,1)S(1)} %qext.1.refs_1_), channel_id=1, source_target_pairs={{0,17},{1,16},{2,19},{3,18},{4,21},{5,20},{6,23},{7,22},{8,25},{9,... | collective-permute-start | bytes 405512 | tf_op jit(solution)/shard_map/ppermute | solution.py:59
  32.0 10.1 %collective-permute-start.3 = (bf16[1040,128]{1,0:T(8,128)(2,1)S(1)}, bf16[1040,128]{1,0:T(8,128)(2,1)S(1)}, u32[]{:S(2)}, u32[]{:S(2)}) collective-permute-start(bf16[1040,128]{1,0:T(8,128)(2,1)S(1)} %prep.1.refs_5_), channel_id=1, source_target_pairs={{0,64},{1,65},{2,66},{3,67},{4,68},{5,69},{6,70},{7,71},{8,72},{9,... | collective-permute-start | bytes 798728 | tf_op jit(solution)/shard_map/ppermute | solution.py:59
  35.3 9.4 %collective-permute-start.6 = (bf16[1040,128]{1,0:T(8,128)(2,1)S(1)}, bf16[1040,128]{1,0:T(8,128)(2,1)S(1)}, u32[]{:S(2)}, u32[]{:S(2)}) collective-permute-start(bf16[1040,128]{1,0:T(8,128)(2,1)S(1)} %prep.1.refs_5_), channel_id=1, source_target_pairs={{0,448},{1,449},{2,450},{3,451},{4,452},{5,453},{6,454},{7,455},{8... | collective-permute-start | bytes 798728 | tf_op jit(solution)/shard_map/ppermute | solution.py:59
  42.2 10.4 %collective-permute-start.4 = (bf16[1040,128]{1,0:T(8,128)(2,1)S(1)}, bf16[1040,128]{1,0:T(8,128)(2,1)S(1)}, u32[]{:S(2)}, u32[]{:S(2)}) collective-permute-start(bf16[1040,128]{1,0:T(8,128)(2,1)S(1)} %collective-permute-done.3.refs_5_), channel_id=1, source_target_pairs={{0,64},{1,65},{2,66},{3,67},{4,68},{5,69},{6,70},{7,71},{8,72},{9,... | collective-permute-start | bytes 798728 | tf_op jit(solution)/shard_map/ppermute | solution.py:59
  44.6 9.9 %collective-permute-start.7 = (bf16[1040,128]{1,0:T(8,128)(2,1)S(1)}, bf16[1040,128]{1,0:T(8,128)(2,1)S(1)}, u32[]{:S(2)}, u32[]{:S(2)}) collective-permute-start(bf16[1040,128]{1,0:T(8,128)(2,1)S(1)} %collective-permute-done.6.refs_6_), channel_id=1, source_target_pairs={{0,448},{1,449},{2,450},{3,451},{4,452},{5,453},{6,454},{7,455},{8... | collective-permute-start | bytes 798728 | tf_op jit(solution)/shard_map/ppermute | solution.py:59
  52.6 10.8 %collective-permute-start.5 = (bf16[1040,128]{1,0:T(8,128)(2,1)S(1)}, bf16[1040,128]{1,0:T(8,128)(2,1)S(1)}, u32[]{:S(2)}, u32[]{:S(2)}) collective-permute-start(bf16[1040,128]{1,0:T(8,128)(2,1)S(1)} %collective-permute-done.4.refs_5_), channel_id=1, source_target_pairs={{0,64},{1,65},{2,66},{3,67},{4,68},{5,69},{6,70},{7,71},{8,72},{9,... | collective-permute-start | bytes 798728 | tf_op jit(solution)/shard_map/ppermute | solution.py:59
  54.5 8.9 %collective-permute-start.8 = (bf16[1040,128]{1,0:T(8,128)(2,1)S(1)}, bf16[1040,128]{1,0:T(8,128)(2,1)S(1)}, u32[]{:S(2)}, u32[]{:S(2)}) collective-permute-start(bf16[1040,128]{1,0:T(8,128)(2,1)S(1)} %collective-permute-done.7.refs_6_), channel_id=1, source_target_pairs={{0,448},{1,449},{2,450},{3,451},{4,452},{5,453},{6,454},{7,455},{8... | collective-permute-start | bytes 798728 | tf_op jit(solution)/shard_map/ppermute | solution.py:59
  63.5 8.4 %collective-permute-start.9 = (bf16[1040,128]{1,0:T(8,128)(2,1)S(1)}, bf16[1040,128]{1,0:T(8,128)(2,1)S(1)}, u32[]{:S(2)}, u32[]{:S(2)}) collective-permute-start(bf16[1040,128]{1,0:T(8,128)(2,1)S(1)} %broadcast_select_fusion), channel_id=1, source_target_pairs={{0,64},{1,65},{2,66},{3,67},{4,68},{5,69},{6,70},{7,71},{8,72},{9,... | collective-permute-start | bytes 798728 | tf_op jit(solution)/shard_map/ppermute | solution.py:59

commit v2 on v1

--- a/solution.py
+++ b/solution.py
@@ -49,10 +49,9 @@
 
 UP = pairs(lambda y, zh, c, x, zl: (y + 1, zh, c, x, zl))
 DOWN = pairs(lambda y, zh, c, x, zl: (y - 1, zh, c, x, zl))
-LAST = pairs(lambda y, zh, c, x, zl: (y + 1 - 2 * c, zh, c, x, zl))
+LAST = pairs(lambda y, zh, c, x, zl: (y + 2 - 4 * c, zh, c, x, zl))
 CORE = pairs(lambda y, zh, c, x, zl: (y, zh, 1 - c, x, zl))
 ZPAIR = pairs(lambda y, zh, c, x, zl: (y, zh, c, x, zl ^ 1))
-DIAG = pairs(lambda y, zh, c, x, zl: (y, zh, 1 - c, x, zl ^ 1))
 
 
 def send(value, perm):
@@ -65,7 +64,7 @@
     return pl.pallas_call(
         kernel,
         out_shape=out,
-        in_specs=[sm if s == "s" else vm for s in in_spaces],
+        in_specs=[{"s": sm, "v": vm, "h": pl.BlockSpec(memory_space=pltpu.HBM)}[s] for s in in_spaces],
         out_specs=jax.tree.map(lambda _: vm, out),
         scratch_shapes=list(scratch),
         input_output_aliases=alias or {},
@@ -75,13 +74,32 @@
     )
 
 
-def pack_kernel(pos_ref, k_ref, v_ref, o_ref):
-    tile = jnp.full((16, DH), pos_ref[0].astype(jnp.float32), jnp.float32).astype(jnp.bfloat16)
+def pack_kernel(pos_hbm, k_hbm, v_hbm, q_hbm, o_ref, q_ref, pos, k_ref, v_ref, sems):
+    copies = [
+        pltpu.make_async_copy(src, dst, sems.at[i])
+        for i, (src, dst) in enumerate(
+            [(pos_hbm, pos), (k_hbm, k_ref), (v_hbm, v_ref), (q_hbm, q_ref.at[pl.ds(0, 512)])]
+        )
+    ]
+    for c in copies:
+        c.start()
+    copies[0].wait()
+    x = lax.axis_index("col") // NZL
+    mine = pos[pl.multiple_of(x * STRIPE, STRIPE)] // STRIPE
+    tile = jnp.full((8, DH), mine.astype(jnp.float32), jnp.float32).astype(jnp.bfloat16)
     for m in range(16):
-        x = (m // 2) % 4
-        o_ref[m, 0:32, :] = k_ref[:, x * DH : (x + 1) * DH]
-        o_ref[m, 32:64, :] = v_ref[:, x * DH : (x + 1) * DH]
-        o_ref[m, 64:80, :] = tile
+        o_ref[m, 64:72, :] = tile
+    row = lax.broadcasted_iota(jnp.int32, (16, DH), 0)
+    tile = jnp.zeros((16, DH), jnp.float32)
+    for r in range(4):
+        tile = jnp.where(row == r, (pos[r * STRIPE] // STRIPE).astype(jnp.float32), tile)
+    q_ref[512:528, :] = tile.astype(jnp.bfloat16)
+    for at, ref, c in ((0, k_ref, copies[1]), (32, v_ref, copies[2])):
+        c.wait()
+        for m in range(16):
+            head = (m // 2) % 4
+            o_ref[m, at : at + 32, :] = ref[:, head * DH : (head + 1) * DH]
+    copies[3].wait()
 
 
 def scalar_of(row):
@@ -114,23 +132,13 @@
     o_ref[2 * BK : ROWS, :] = tile.astype(jnp.bfloat16)
 
 
-def qext_kernel(pos_ref, q_ref, o_ref):
-    o_ref[0:512, :] = q_ref[...]
-    row = lax.broadcasted_iota(jnp.int32, (16, DH), 0)
-    tile = jnp.zeros((16, DH), jnp.float32)
-    for r in range(4):
-        tile = jnp.where(row == r, pos_ref[r].astype(jnp.float32), tile)
-    o_ref[512:528, :] = tile.astype(jnp.bfloat16)
-
-
-def attend_kernel(nblocks, first, side_ref, qo_ref, qz_ref, qc_ref, qd_ref, *rest):
-    blocks = rest[:nblocks]
-    if first:
-        acc_ref, m_ref, q_ref, off_ref, qp, qt, kp = rest[nblocks:]
-        accin_ref = min_ref = None
-    else:
-        accin_ref, min_ref, acc_ref, m_ref, q_ref, off_ref, qp, qt, kp = rest[nblocks:]
-    side = side_ref[0]
+def attend_kernel(nblocks, first, last, qo_ref, qz_ref, qc_ref, qd_ref, *rest):
+    blocks, rest = rest[:nblocks], list(rest[nblocks:])
+    accin_ref, min_ref = (None, None) if first else (rest.pop(0), rest.pop(0))
+    out_ref = rest.pop(0) if last else None
+    acc_ref, m_ref, q_ref, off_ref, qp, qt, kp = rest
+    core = lax.axis_index("blk") % NC
+    side = lax.axis_index("col") % 2
     pos = []
     for t in range(4):
         q_ref[t, 0:128, :] = qo_ref[t * 128 : (t + 1) * 128, :]
@@ -150,73 +158,85 @@
     for n, blk in enumerate(blocks):
         for j in range(NST):
             kp[n * NST + j] = scalar_of(blk[2 * BK + j : 2 * BK + j + 1, :])
-    r = lax.broadcasted_iota(jnp.int32, (SUB, 256), 0)
-    lane = lax.broadcasted_iota(jnp.int32, (SUB, 256), 1)
-    off_ref[...] = (r // 32) * 64 + side * 32 + r % 32 - lane % 128
-    ones = jnp.ones((16, BK), jnp.bfloat16)
     if first:
+        r = lax.broadcasted_iota(jnp.int32, (SUB, 256), 0)
+        lane = lax.broadcasted_iota(jnp.int32, (SUB, 256), 1)
+        off = (r // 32) * 64 + side * 32 + r % 32 - lane % 128
+        off_ref[0] = jnp.zeros((SUB, 256), jnp.float32)
+        off_ref[1] = jnp.where(off <= 0, 0.0, MASKED)
         acc_ref[...] = jnp.zeros_like(acc_ref)
         m_ref[...] = jnp.full(m_ref.shape, EMPTY, jnp.float32)
     else:
         acc_ref[...] = accin_ref[...]
         m_ref[...] = min_ref[...]
-
-    def local(qpos, t, keys):
-        scores = []
-        for n, blk in enumerate(blocks):
-            s = lax.dot_general(
-                blk[0:keys, :], q_ref[t], (((1,), (1,)), ((), ())), preferred_element_type=jnp.float32
-            )
-            parts = []
+    ones = jnp.ones((16, BK), jnp.bfloat16)
+
+    def scores(t, keys):
+        return [
+            lax.dot_general(blk[0:keys, :], q_ref[t], (((1,), (1,)), ((), ())), preferred_element_type=jnp.float32)
+            for blk in blocks
+        ]
+
+    def local(qpos, raw, keys):
+        parts = []
+        top = None
+        for n, s in enumerate(raw):
+            runs = []
             for j in range(keys // SUB):
-                gap = (qpos - kp[n * NST + j]) * STRIPE
-                parts.append(jnp.where(off_ref[...] <= gap, s[j * SUB : (j + 1) * SUB, :] * C2, MASKED))
-            scores.append(jnp.concatenate(parts, axis=0))
-        top = jnp.max(scores[0], axis=0, keepdims=True)
-        for s in scores[1:]:
-            top = jnp.maximum(top, jnp.max(s, axis=0, keepdims=True))
+                run = s[j * SUB : (j + 1) * SUB, :]
+                kpos = kp[n * NST + j]
+                if first:
+                    run = run + off_ref[(kpos == qpos).astype(jnp.int32)]
+                hidden = jnp.where(kpos <= qpos, 0.0, MASKED).astype(jnp.float32)
+                high = jnp.max(run.reshape(SUB // 8, 8, 256), axis=0) * C2 + hidden
+                top = high if top is None else jnp.maximum(top, high)
+                runs.append((run, hidden))
+            parts.append(runs)
+        top = jnp.maximum(jnp.max(top, axis=0, keepdims=True), EMPTY)
         mixed = None
-        for s, blk in zip(scores, blocks):
-            p = jnp.exp2(s - top).astype(jnp.bfloat16)
+        for runs, blk in zip(parts, blocks):
+            p = jnp.concatenate([jnp.exp2(run * C2 + (hidden - top)) for run, hidden in runs], axis=0)
             vt = jnp.concatenate(
                 [blk[BK + i * DH : BK + (i + 1) * DH, :] for i in range(keys // DH)], axis=1
             )
             vt = jnp.concatenate([vt, ones[:, 0:keys]], axis=0)
-            part = jnp.dot(vt, p, preferred_element_type=jnp.float32)
+            part = jnp.dot(vt, p.astype(jnp.bfloat16), preferred_element_type=jnp.float32)
             mixed = part if mixed is None else mixed + part
         return top, mixed
 
-    def two(i, keys):
-        found = [(qt[2 * i + k],) + local(qp[2 * i + k], qt[2 * i + k], keys) for k in range(2)]
+    size = 2
+
+    def together(i, keys):
+        raws = [scores(qt[size * i + k], keys) for k in range(size)]
+        found = [(qt[size * i + k],) + local(qp[size * i + k], raws[k], keys) for k in range(size)]
         for t, top, mixed in found:
             old = m_ref[t, 0:1, :]
             new = jnp.maximum(old, top)
             acc_ref[t] = acc_ref[t] * jnp.exp2(old - new) + mixed * jnp.exp2(top - new)
             m_ref[t] = jnp.broadcast_to(new, (8, 256))
 
-    def pair(i, carry):
-        far = qp[2 * i + 1]
-        wide = kp[NST // 2] <= far
-        seen = kp[0] <= far
-        for n in range(1, nblocks):
-            wide = jnp.logical_or(wide, kp[n * NST + NST // 2] <= far)
-            seen = jnp.logical_or(seen, kp[n * NST] <= far)
-
-        @pl.when(wide)
-        def _():
-            two(i, BK)
-
-        @pl.when(jnp.logical_and(seen, jnp.logical_not(wide)))
-        def _():
-            two(i, BK // 2)
+    def group(i, carry):
+        far = qp[size * i + size - 1]
+        need = jnp.int32(0)
+        for n in range(nblocks):
+            seen = jnp.int32(0)
+            for j in (0, 4, 6):
+                seen = seen + (kp[n * NST + j] <= far).astype(jnp.int32)
+            need = jnp.maximum(need, seen)
+        for level, keys in ((1, 4 * SUB), (2, 6 * SUB), (3, 8 * SUB)):
+
+            @pl.when(need == level)
+            def _(keys=keys):
+                together(i, keys)
 
         return carry
 
-    lax.fori_loop(0, NQ // 2, pair, 0)
-
-
-def partial_kernel(who_ref, acc_ref, m_ref, o_ref):
-    core, side = who_ref[0], who_ref[1]
+    lax.fori_loop(0, NQ // size, group, 0)
+    if last:
+        partial(core, side, acc_ref, m_ref, out_ref)
+
+
+def partial(core, side, acc_ref, m_ref, o_ref):
     for dc in range(2):
         for dz in range(2):
             member = (core + dc - 2 * core * dc) * 2 + (side + dz - 2 * side * dz)
@@ -260,15 +280,24 @@
 
 def body(queries, keys, values, positions):
     bf, f32 = jnp.bfloat16, jnp.float32
-    blk, col = lax.axis_index("blk"), lax.axis_index("col")
-    core, side, x = blk % 2, col % 2, col // 4
-    stripes = positions.reshape(4, STRIPE)[:, 0] // STRIPE
-    mine = lax.dynamic_slice_in_dim(stripes, x, 1)
-    who = jnp.stack([core, side]).astype(jnp.int32)
-    side_arr = side.reshape(1).astype(jnp.int32)
-
-    packed = call(pack_kernel, jax.ShapeDtypeStruct((16, 80, DH), bf), "svv", name="pack")(mine, keys, values)
+    core = lax.axis_index("blk") % NC
+
+    packed, qo = call(
+        pack_kernel,
+        (jax.ShapeDtypeStruct((16, 72, DH), bf), jax.ShapeDtypeStruct((528, DH), bf)),
+        "hhhh",
+        scratch=[
+            SM((512,), jnp.int32),
+            VM((32, HK * DH), bf),
+            VM((32, HK * DH), bf),
+            pltpu.SemaphoreType.DMA((4,)),
+        ],
+        name="pack",
+    )(*[pltpu.with_memory_space_constraint(a, pltpu.HBM) for a in (positions, keys, values, queries)])
     got = lax.all_to_all(packed, ("blk", "col"), 0, 0, axis_index_groups=KV_GROUPS, tiled=False)
+    qz, qc = send(qo, ZPAIR), send(qo, CORE)
+    qd = send(qz, CORE)
+    qs = (qo, qz, qc, qd)
     own = call(
         prep_kernel,
         jax.ShapeDtypeStruct((ROWS, DH), bf),
@@ -276,45 +305,44 @@
         scratch=[VM((BK, DH), f32), SM((NST,), jnp.int32)],
         name="prep",
     )(got)
-    qo = call(qext_kernel, jax.ShapeDtypeStruct((528, DH), bf), "sv", name="qext")(stripes, queries)
 
     up, down = [send(own, UP)], [send(own, DOWN)]
-    qc, qz, qd = send(qo, CORE), send(qo, ZPAIR), send(qo, DIAG)
-    qs = (side_arr, qo, qz, qc, qd)
     for step in range(2):
         up.append(send(up[-1], UP))
         down.append(send(down[-1], DOWN))
-    last = send(jnp.where(core == 0, up[2], down[2]), LAST)
-
-    state = (jax.ShapeDtypeStruct((NQ, 144, 256), f32), jax.ShapeDtypeStruct((NQ, 8, 256), f32))
-
-    def attend(blocks, carry):
+    far = send(jnp.where(core == 0, up[1], down[1]), LAST)
+
+    acc = jax.ShapeDtypeStruct((NQ, 144, 256), f32)
+    top = jax.ShapeDtypeStruct((NQ, 8, 256), f32)
+
+    def attend(blocks, carry, last=False):
         n = len(blocks)
         first = carry is None
-        kernel = lambda *refs: attend_kernel(n, first, *refs)
+        kernel = lambda *refs: attend_kernel(n, first, last, *refs)
         scratch = [
             VM((NQ, 256, DH), bf),
-            VM((SUB, 256), jnp.int32),
+            VM((2, SUB, 256), f32),
             SM((NQ,), jnp.int32),
             SM((NQ,), jnp.int32),
-            SM((2 * NST,), jnp.int32),
+            SM((n * NST,), jnp.int32),
         ]
+        if last:
+            scratch = [VM(acc.shape, f32), VM(top.shape, f32)] + scratch
         args = qs + tuple(blocks) + (() if first else carry)
         return call(
             kernel,
-            state,
-            "svvvv" + "v" * (n + (0 if first else 2)),
+            jax.ShapeDtypeStruct((4, 528, DH), bf) if last else (acc, top),
+            "v" * len(args),
             scratch=scratch,
-            alias=None if first else {5 + n: 0, 6 + n: 1},
+            alias=None if first or last else {4 + n: 0, 5 + n: 1},
             flops=n * 2_000_000_000,
             name=f"attend{n}",
         )(*args)
 
     carry = attend([own], None)
-    for a, b in zip(up, down):
-        carry = attend([a, b], carry)
-    carry = attend([last], carry)
-    part = call(partial_kernel, jax.ShapeDtypeStruct((4, 528, DH), bf), "svv", name="partial")(who, *carry)
+    carry = attend([up[0], down[0]], carry)
+    carry = attend([up[1], down[1]], carry)
+    part = attend([up[2], down[2], far], carry, last=True)
     parts = lax.all_to_all(part, ("blk", "col"), 0, 0, axis_index_groups=OUT_GROUPS, tiled=False)
     attended, lognorm = call(
         merge_kernel,

time: 96.8 us -> 90.3 us (0.933)
  the two profiles are of different devices: /device:TPU:1 before, /device:TPU:6 now
where the time goes in v2:
time: 90.3 us; the launch traced here: 89.8 us
  starting transfers between devices  47.4 us (52%)
  Pallas kernels  17.4 us (19%)
  waiting for transfers between devices  12.7 us (14%)
  blocking collectives  11.4 us (13%)
    ppermute x10, starting transfers between devices, send(): return lax.ppermute(value, ('blk', 'col'), perm)  34.2 us
    pallas_call x4, Pallas kernels, attend(): call(kernel, jax.ShapeDtypeStruct((4, 528, DH), bf) if last else (acc, to...  14.4 us
    all_to_all x1, starting transfers between devices, body(): lax.all_to_all(packed, ('blk', 'col'), 0, 0, axis_index_groups=KV_GROUPS,...  13.3 us
    ppermute x10, waiting for transfers between devices, send(): return lax.ppermute(value, ('blk', 'col'), perm)  12.7 us
    all_to_all x1, blocking collectives, body(): lax.all_to_all(part, ('blk', 'col'), 0, 0, axis_index_groups=OUT_GROUPS,...  11.4 us
  transfers between devices with their start and end apart: 11, of which 5 were waited for; matrix products, arithmetic and copies ran while one was open for 0% of the time, Pallas kernels for 11%

profile of v2, /device:TPU:6, one launch (start us, length us, event | category | flops | bytes accessed | tf_op | source)
XLA Modules:
  0.0 89.8 jit_solution(17524715385414380094)
XLA Ops:
  0.6 1.7 %pack.1 = (bf16[16,72,128]{2,1,0:T(8,128)(2,1)}, bf16[528,128]{1,0:T(8,128)(2,1)S(1)}) custom-call(s32[512]{0:T(512)} %pos_hbm.1, bf16[32,512]{1,0:T(8,128)(2,1)} %k_hbm.1, bf16[32,512]{1,0:T(8,128)(2,1)} %v_hbm.1, bf16[512,128]{1,0:T(8,128)(2,1)} %q_hbm.1), custom_call_target="tpu_custom_call" | custom-call | tf_op jit(solution)/shard_map/pack/pallas_call | solution.py:285
  2.3 13.3 %all-to-all-start = ((bf16[16,72,128]{2,1,0:T(8,128)(2,1)}), bf16[16,72,128]{2,1,0:T(8,128)(2,1)S(1)}, u32[]{:S(2)}, u32[]{:S(2)}) async-start(bf16[16,72,128]{2,1,0:T(8,128)(2,1)} %get-tuple-element.13), calls=%async_computation | async-start | bytes 589824 | tf_op jit(solution)/shard_map/all_to_all | solution.py:297
  15.6 3.4 %collective-permute-start = (bf16[528,128]{1,0:T(8,128)(2,1)S(1)}, bf16[528,128]{1,0:T(8,128)(2,1)S(1)}, u32[]{:S(2)}, u32[]{:S(2)}) collective-permute-start(bf16[528,128]{1,0:T(8,128)(2,1)S(1)} %get-tuple-element.12.refs_0_), channel_id=1, source_target_pairs={{0,1},{1,0},{2,3},{3,2},{4,5},{5,4},{6,7},{7,6},{8,9},{9,8},{10,11... | collective-permute-start | bytes 405512 | tf_op jit(solution)/shard_map/ppermute | solution.py:58
  19.0 1.9 %collective-permute-start.1 = (bf16[528,128]{1,0:T(8,128)(2,1)S(1)}, bf16[528,128]{1,0:T(8,128)(2,1)S(1)}, u32[]{:S(2)}, u32[]{:S(2)}) collective-permute-start(bf16[528,128]{1,0:T(8,128)(2,1)S(1)} %get-tuple-element.12.refs_0_), channel_id=1, source_target_pairs={{0,16},{1,17},{2,18},{3,19},{4,20},{5,21},{6,22},{7,23},{8,24},{9,... | collective-permute-start | bytes 405512 | tf_op jit(solution)/shard_map/ppermute | solution.py:58
  20.9 5.7 %collective-permute-done.refs_1_ = bf16[528,128]{1,0:T(8,128)(2,1)S(1)} collective-permute-done((bf16[528,128]{1,0:T(8,128)(2,1)S(1)}, bf16[528,128]{1,0:T(8,128)(2,1)S(1)}, u32[]{:S(2)}, u32[]{:S(2)}) %collective-permute-start) | collective-permute-done | bytes 135200 | tf_op jit(solution)/shard_map/ppermute | solution.py:58
  26.6 1.9 %collective-permute-start.2 = (bf16[528,128]{1,0:T(8,128)(2,1)S(1)}, bf16[528,128]{1,0:T(8,128)(2,1)S(1)}, u32[]{:S(2)}, u32[]{:S(2)}) collective-permute-start(bf16[528,128]{1,0:T(8,128)(2,1)S(1)} %collective-permute-done.refs_1_), channel_id=1, source_target_pairs={{0,16},{1,17},{2,18},{3,19},{4,20},{5,21},{6,22},{7,23},{8,24},{9,... | collective-permute-start | bytes 405512 | tf_op jit(solution)/shard_map/ppermute | solution.py:58
  28.5 0.3 prep.1.refs_4_
  28.9 3.5 %collective-permute-start.3 = (bf16[1040,128]{1,0:T(8,128)(2,1)S(1)}, bf16[1040,128]{1,0:T(8,128)(2,1)S(1)}, u32[]{:S(2)}, u32[]{:S(2)}) collective-permute-start(bf16[1040,128]{1,0:T(8,128)(2,1)S(1)} %prep.1.refs_4_), channel_id=1, source_target_pairs={{0,64},{1,65},{2,66},{3,67},{4,68},{5,69},{6,70},{7,71},{8,72},{9,... | collective-permute-start | bytes 798728 | tf_op jit(solution)/shard_map/ppermute | solution.py:58
  32.4 3.8 %collective-permute-start.6 = (bf16[1040,128]{1,0:T(8,128)(2,1)S(1)}, bf16[1040,128]{1,0:T(8,128)(2,1)S(1)}, u32[]{:S(2)}, u32[]{:S(2)}) collective-permute-start(bf16[1040,128]{1,0:T(8,128)(2,1)S(1)} %prep.1.refs_4_), channel_id=1, source_target_pairs={{0,448},{1,449},{2,450},{3,451},{4,452},{5,453},{6,454},{7,455},{8... | collective-permute-start | bytes 798728 | tf_op jit(solution)/shard_map/ppermute | solution.py:58
  36.2 2.6 %attend1.1 = (f32[8,144,256]{2,1,0:T(8,128)S(1)}, f32[8,8,256]{2,1,0:T(8,128)S(1)}) custom-call(bf16[528,128]{1,0:T(8,128)(2,1)S(1)} %get-tuple-element.12.refs_0_, bf16[528,128]{1,0:T(8,128)(2,1)S(1)} %collective-permute-done.refs_1_, bf16[528,128]{1,0:T(8,128)(2,1)S(1)} %collective-permute-done.1.refs_2_, ...), custom_call_target="tpu_custom_call" | custom-call | flops 2000000000 | tf_op jit(solution)/shard_map/attend1/pallas_call | solution.py:332
  38.8 2.5 %collective-permute-done.3.refs_4_ = bf16[1040,128]{1,0:T(8,128)(2,1)S(1)} collective-permute-done((bf16[1040,128]{1,0:T(8,128)(2,1)S(1)}, bf16[1040,128]{1,0:T(8,128)(2,1)S(1)}, u32[]{:S(2)}, u32[]{:S(2)}) %collective-permute-start.3) | collective-permute-done | bytes 266272 | tf_op jit(solution)/shard_map/ppermute | solution.py:58
  41.3 1.9 %collective-permute-start.4 = (bf16[1040,128]{1,0:T(8,128)(2,1)S(1)}, bf16[1040,128]{1,0:T(8,128)(2,1)S(1)}, u32[]{:S(2)}, u32[]{:S(2)}) collective-permute-start(bf16[1040,128]{1,0:T(8,128)(2,1)S(1)} %collective-permute-done.3.refs_4_), channel_id=1, source_target_pairs={{0,64},{1,65},{2,66},{3,67},{4,68},{5,69},{6,70},{7,71},{8,72},{9,... | collective-permute-start | bytes 798728 | tf_op jit(solution)/shard_map/ppermute | solution.py:58
  43.2 5.1 %collective-permute-start.7 = (bf16[1040,128]{1,0:T(8,128)(2,1)S(1)}, bf16[1040,128]{1,0:T(8,128)(2,1)S(1)}, u32[]{:S(2)}, u32[]{:S(2)}) collective-permute-start(bf16[1040,128]{1,0:T(8,128)(2,1)S(1)} %collective-permute-done.6.refs_5_), channel_id=1, source_target_pairs={{0,448},{1,449},{2,450},{3,451},{4,452},{5,453},{6,454},{7,455},{8... | collective-permute-start | bytes 798728 | tf_op jit(solution)/shard_map/ppermute | solution.py:58
  48.4 3.5 %attend2.2 = (f32[8,144,256]{2,1,0:T(8,128)S(1)}, f32[8,8,256]{2,1,0:T(8,128)S(1)}) custom-call(bf16[528,128]{1,0:T(8,128)(2,1)S(1)} %get-tuple-element.12.refs_0_, bf16[528,128]{1,0:T(8,128)(2,1)S(1)} %collective-permute-done.refs_1_, bf16[528,128]{1,0:T(8,128)(2,1)S(1)} %collective-permute-done.1.refs_2_, ...), custom_call_target="tpu_custom_call", output_to_operand_aliasing={{0}: (6, {}), {1}: (7, {})} | custom-call | flops 4000000000 | tf_op jit(solution)/shard_map/attend2/pallas_call | solution.py:332
  51.9 0.7 collective-permute-done.4.refs_4_
  52.6 1.2 %collective-permute-done.7.refs_5_ = bf16[1040,128]{1,0:T(8,128)(2,1)S(1)} collective-permute-done((bf16[1040,128]{1,0:T(8,128)(2,1)S(1)}, bf16[1040,128]{1,0:T(8,128)(2,1)S(1)}, u32[]{:S(2)}, u32[]{:S(2)}) %collective-permute-start.7) | collective-permute-done | bytes 266272 | tf_op jit(solution)/shard_map/ppermute | solution.py:58
  53.8 5.6 %collective-permute-start.9 = (bf16[1040,128]{1,0:T(8,128)(2,1)S(1)}, bf16[1040,128]{1,0:T(8,128)(2,1)S(1)}, u32[]{:S(2)}, u32[]{:S(2)}) collective-permute-start(bf16[1040,128]{1,0:T(8,128)(2,1)S(1)} %broadcast_select_fusion), channel_id=1, source_target_pairs={{0,128},{1,129},{2,130},{3,131},{4,132},{5,133},{6,134},{7,135},{8... | collective-permute-start | bytes 798728 | tf_op jit(solution)/shard_map/ppermute | solution.py:58
  59.4 4.9 %collective-permute-start.5 = (bf16[1040,128]{1,0:T(8,128)(2,1)S(1)}, bf16[1040,128]{1,0:T(8,128)(2,1)S(1)}, u32[]{:S(2)}, u32[]{:S(2)}) collective-permute-start(bf16[1040,128]{1,0:T(8,128)(2,1)S(1)} %collective-permute-done.4.refs_4_), channel_id=1, source_target_pairs={{0,64},{1,65},{2,66},{3,67},{4,68},{5,69},{6,70},{7,71},{8,72},{9,... | collective-permute-start | bytes 798728 | tf_op jit(solution)/shard_map/ppermute | solution.py:58
  64.3 2.2 %collective-permute-start.8 = (bf16[1040,128]{1,0:T(8,128)(2,1)S(1)}, bf16[1040,128]{1,0:T(8,128)(2,1)S(1)}, u32[]{:S(2)}, u32[]{:S(2)}) collective-permute-start(bf16[1040,128]{1,0:T(8,128)(2,1)S(1)} %collective-permute-done.7.refs_5_), channel_id=1, source_target_pairs={{0,448},{1,449},{2,450},{3,451},{4,452},{5,453},{6,454},{7,455},{8... | collective-permute-start | bytes 798728 | tf_op jit(solution)/shard_map/ppermute | solution.py:58
  66.5 3.5 %attend2.3 = (f32[8,144,256]{2,1,0:T(8,128)S(1)}, f32[8,8,256]{2,1,0:T(8,128)S(1)}) custom-call(bf16[528,128]{1,0:T(8,128)(2,1)S(1)} %get-tuple-element.12.refs_0_, bf16[528,128]{1,0:T(8,128)(2,1)S(1)} %collective-permute-done.refs_1_, bf16[528,128]{1,0:T(8,128)(2,1)S(1)} %collective-permute-done.1.refs_2_, ...), custom_call_target="tpu_custom_call", output_to_operand_aliasing={{0}: (6, {}), {1}: (7, {})} | custom-call | flops 4000000000 | tf_op jit(solution)/shard_map/attend2/pallas_call | solution.py:332
  70.0 2.6 %collective-permute-done.5.refs_4_ = bf16[1040,128]{1,0:T(8,128)(2,1)S(1)} collective-permute-done((bf16[1040,128]{1,0:T(8,128)(2,1)S(1)}, bf16[1040,128]{1,0:T(8,128)(2,1)S(1)}, u32[]{:S(2)}, u32[]{:S(2)}) %collective-permute-start.5) | collective-permute-done | bytes 266272 | tf_op jit(solution)/shard_map/ppermute | solution.py:58
  72.6 4.7 %attend3.1 = bf16[4,528,128]{2,1,0:T(8,128)(2,1)S(1)} custom-call(bf16[528,128]{1,0:T(8,128)(2,1)S(1)} %get-tuple-element.12.refs_0_, bf16[528,128]{1,0:T(8,128)(2,1)S(1)} %collective-permute-done.refs_1_, bf16[528,128]{1,0:T(8,128)(2,1)S(1)} %collective-permute-done.1.refs_2_, bf16[528,128]{1,0:T(8,128)(2,1)S(1)} %collective-permute-done.2.refs_3_, ...), custom_call_target="tpu_custom_call" | custom-call | flops 6000000000 | tf_op jit(solution)/shard_map/attend3/pallas_call | solution.py:332
  77.3 11.4 %all_to_all.10.i_ref = bf16[4,528,128]{2,1,0:T(8,128)(2,1)S(1)} all-to-all(bf16[4,528,128]{2,1,0:T(8,128)(2,1)S(1)} %attend3.1), channel_id=1, replica_groups={{0,1,16,17},{2,3,18,19},{4,5,20,21},{6,7,22,23},{8,9,24,25},{10,11,26,2..., dimensions={0} | all-to-all | bytes 1081344 | tf_op jit(solution)/shard_map/all_to_all | solution.py:346
  88.7 1.1 %merge.1 = (f32[512,128]{1,0:T(8,128)}, f32[4,128]{1,0:T(4,128)}) custom-call(bf16[4,528,128]{2,1,0:T(8,128)(2,1)S(1)} %all_to_all.10.i_ref), custom_call_target="tpu_custom_call" | custom-call | tf_op jit(solution)/shard_map/merge/pallas_call | solution.py:347
  (7 shorter events, 0.1 us)
Async XLA Ops:
  2.3 26.2 %all-to-all-start = ((bf16[16,72,128]{2,1,0:T(8,128)(2,1)}), bf16[16,72,128]{2,1,0:T(8,128)(2,1)S(1)}, u32[]{:S(2)}, u32[]{:S(2)}) async-start(bf16[16,72,128]{2,1,0:T(8,128)(2,1)} %get-tuple-element.13), calls=%async_computation | async-start | bytes 589824 | tf_op jit(solution)/shard_map/all_to_all | solution.py:297
  15.6 11.0 %collective-permute-start = (bf16[528,128]{1,0:T(8,128)(2,1)S(1)}, bf16[528,128]{1,0:T(8,128)(2,1)S(1)}, u32[]{:S(2)}, u32[]{:S(2)}) collective-permute-start(bf16[528,128]{1,0:T(8,128)(2,1)S(1)} %get-tuple-element.12.refs_0_), channel_id=1, source_target_pairs={{0,1},{1,0},{2,3},{3,2},{4,5},{5,4},{6,7},{7,6},{8,9},{9,8},{10,11... | collective-permute-start | bytes 405512 | tf_op jit(solution)/shard_map/ppermute | solution.py:58
  19.0 17.2 %collective-permute-start.1 = (bf16[528,128]{1,0:T(8,128)(2,1)S(1)}, bf16[528,128]{1,0:T(8,128)(2,1)S(1)}, u32[]{:S(2)}, u32[]{:S(2)}) collective-permute-start(bf16[528,128]{1,0:T(8,128)(2,1)S(1)} %get-tuple-element.12.refs_0_), channel_id=1, source_target_pairs={{0,16},{1,17},{2,18},{3,19},{4,20},{5,21},{6,22},{7,23},{8,24},{9,... | collective-permute-start | bytes 405512 | tf_op jit(solution)/shard_map/ppermute | solution.py:58
  26.6 9.6 %collective-permute-start.2 = (bf16[528,128]{1,0:T(8,128)(2,1)S(1)}, bf16[528,128]{1,0:T(8,128)(2,1)S(1)}, u32[]{:S(2)}, u32[]{:S(2)}) collective-permute-start(bf16[528,128]{1,0:T(8,128)(2,1)S(1)} %collective-permute-done.refs_1_), channel_id=1, source_target_pairs={{0,16},{1,17},{2,18},{3,19},{4,20},{5,21},{6,22},{7,23},{8,24},{9,... | collective-permute-start | bytes 405512 | tf_op jit(solution)/shard_map/ppermute | solution.py:58
  28.9 12.4 %collective-permute-start.3 = (bf16[1040,128]{1,0:T(8,128)(2,1)S(1)}, bf16[1040,128]{1,0:T(8,128)(2,1)S(1)}, u32[]{:S(2)}, u32[]{:S(2)}) collective-permute-start(bf16[1040,128]{1,0:T(8,128)(2,1)S(1)} %prep.1.refs_4_), channel_id=1, source_target_pairs={{0,64},{1,65},{2,66},{3,67},{4,68},{5,69},{6,70},{7,71},{8,72},{9,... | collective-permute-start | bytes 798728 | tf_op jit(solution)/shard_map/ppermute | solution.py:58
  32.4 10.9 %collective-permute-start.6 = (bf16[1040,128]{1,0:T(8,128)(2,1)S(1)}, bf16[1040,128]{1,0:T(8,128)(2,1)S(1)}, u32[]{:S(2)}, u32[]{:S(2)}) collective-permute-start(bf16[1040,128]{1,0:T(8,128)(2,1)S(1)} %prep.1.refs_4_), channel_id=1, source_target_pairs={{0,448},{1,449},{2,450},{3,451},{4,452},{5,453},{6,454},{7,455},{8... | collective-permute-start | bytes 798728 | tf_op jit(solution)/shard_map/ppermute | solution.py:58
  41.3 11.3 %collective-permute-start.4 = (bf16[1040,128]{1,0:T(8,128)(2,1)S(1)}, bf16[1040,128]{1,0:T(8,128)(2,1)S(1)}, u32[]{:S(2)}, u32[]{:S(2)}) collective-permute-start(bf16[1040,128]{1,0:T(8,128)(2,1)S(1)} %collective-permute-done.3.refs_4_), channel_id=1, source_target_pairs={{0,64},{1,65},{2,66},{3,67},{4,68},{5,69},{6,70},{7,71},{8,72},{9,... | collective-permute-start | bytes 798728 | tf_op jit(solution)/shard_map/ppermute | solution.py:58
  43.2 10.6 %collective-permute-start.7 = (bf16[1040,128]{1,0:T(8,128)(2,1)S(1)}, bf16[1040,128]{1,0:T(8,128)(2,1)S(1)}, u32[]{:S(2)}, u32[]{:S(2)}) collective-permute-start(bf16[1040,128]{1,0:T(8,128)(2,1)S(1)} %collective-permute-done.6.refs_5_), channel_id=1, source_target_pairs={{0,448},{1,449},{2,450},{3,451},{4,452},{5,453},{6,454},{7,455},{8... | collective-permute-start | bytes 798728 | tf_op jit(solution)/shard_map/ppermute | solution.py:58
  53.8 16.2 %collective-permute-start.9 = (bf16[1040,128]{1,0:T(8,128)(2,1)S(1)}, bf16[1040,128]{1,0:T(8,128)(2,1)S(1)}, u32[]{:S(2)}, u32[]{:S(2)}) collective-permute-start(bf16[1040,128]{1,0:T(8,128)(2,1)S(1)} %broadcast_select_fusion), channel_id=1, source_target_pairs={{0,128},{1,129},{2,130},{3,131},{4,132},{5,133},{6,134},{7,135},{8... | collective-permute-start | bytes 798728 | tf_op jit(solution)/shard_map/ppermute | solution.py:58
  59.4 13.2 %collective-permute-start.5 = (bf16[1040,128]{1,0:T(8,128)(2,1)S(1)}, bf16[1040,128]{1,0:T(8,128)(2,1)S(1)}, u32[]{:S(2)}, u32[]{:S(2)}) collective-permute-start(bf16[1040,128]{1,0:T(8,128)(2,1)S(1)} %collective-permute-done.4.refs_4_), channel_id=1, source_target_pairs={{0,64},{1,65},{2,66},{3,67},{4,68},{5,69},{6,70},{7,71},{8,72},{9,... | collective-permute-start | bytes 798728 | tf_op jit(solution)/shard_map/ppermute | solution.py:58
  64.3 8.3 %collective-permute-start.8 = (bf16[1040,128]{1,0:T(8,128)(2,1)S(1)}, bf16[1040,128]{1,0:T(8,128)(2,1)S(1)}, u32[]{:S(2)}, u32[]{:S(2)}) collective-permute-start(bf16[1040,128]{1,0:T(8,128)(2,1)S(1)} %collective-permute-done.7.refs_5_), channel_id=1, source_target_pairs={{0,448},{1,449},{2,450},{3,451},{4,452},{5,453},{6,454},{7,455},{8... | collective-permute-start | bytes 798728 | tf_op jit(solution)/shard_map/ppermute | solution.py:58

commit v3 on v2

--- a/solution.py
+++ b/solution.py
@@ -49,7 +49,7 @@
 
 UP = pairs(lambda y, zh, c, x, zl: (y + 1, zh, c, x, zl))
 DOWN = pairs(lambda y, zh, c, x, zl: (y - 1, zh, c, x, zl))
-LAST = pairs(lambda y, zh, c, x, zl: (y + 2 - 4 * c, zh, c, x, zl))
+LAST = pairs(lambda y, zh, c, x, zl: (y + 1 - 2 * c, zh, c, x, zl))
 CORE = pairs(lambda y, zh, c, x, zl: (y, zh, 1 - c, x, zl))
 ZPAIR = pairs(lambda y, zh, c, x, zl: (y, zh, c, x, zl ^ 1))
 
@@ -220,10 +220,10 @@
         need = jnp.int32(0)
         for n in range(nblocks):
             seen = jnp.int32(0)
-            for j in (0, 4, 6):
+            for j in (0, 2, 4, 6):
                 seen = seen + (kp[n * NST + j] <= far).astype(jnp.int32)
             need = jnp.maximum(need, seen)
-        for level, keys in ((1, 4 * SUB), (2, 6 * SUB), (3, 8 * SUB)):
+        for level, keys in ((1, 2 * SUB), (2, 4 * SUB), (3, 6 * SUB), (4, 8 * SUB)):
 
             @pl.when(need == level)
             def _(keys=keys):
@@ -310,7 +310,7 @@
     for step in range(2):
         up.append(send(up[-1], UP))
         down.append(send(down[-1], DOWN))
-    far = send(jnp.where(core == 0, up[1], down[1]), LAST)
+    far = send(jnp.where(core == 0, up[2], down[2]), LAST)
 
     acc = jax.ShapeDtypeStruct((NQ, 144, 256), f32)
     top = jax.ShapeDtypeStruct((NQ, 8, 256), f32)
@@ -342,7 +342,8 @@
     carry = attend([own], None)
     carry = attend([up[0], down[0]], carry)
     carry = attend([up[1], down[1]], carry)
-    part = attend([up[2], down[2], far], carry, last=True)
+    carry = attend([up[2], down[2]], carry)
+    part = attend([far], carry, last=True)
     parts = lax.all_to_all(part, ("blk", "col"), 0, 0, axis_index_groups=OUT_GROUPS, tiled=False)
     attended, lognorm = call(
         merge_kernel,

time: 90.3 us -> 90.5 us (level)
  starting transfers between devices: 47.4 us -> 44.8 us
  waiting for transfers between devices: 12.7 us -> 14.5 us
    ppermute x10, starting transfers between devices: 34.2 us -> 31.5 us  [send(): return lax.ppermute(value, ('blk', 'col'), perm)]
    ppermute x10, waiting for transfers between devices: 12.7 us -> 14.5 us  [send(): return lax.ppermute(value, ('blk', 'col'), perm)]
    pallas_call x4 -> x5, Pallas kernels: 14.4 us -> 14.9 us  [attend(): call(kernel, jax.ShapeDtypeStruct((4, 528, DH), bf) if last else (acc, to...]
  transfers between devices with their start and end apart: 11 -> 11, of which waited for: 5 -> 5; matrix products, arithmetic and copies ran while one was open for 0% -> 0% of each run, Pallas kernels for 11% -> 14%
where the time goes in v3:
time: 90.5 us; the launch traced here: 89.5 us
  starting transfers between devices  44.8 us (50%)
  Pallas kernels  18 us (20%)
  waiting for transfers between devices  14.5 us (16%)
  blocking collectives  11.4 us (13%)
    ppermute x10, starting transfers between devices, send(): return lax.ppermute(value, ('blk', 'col'), perm)  31.5 us
    pallas_call x5, Pallas kernels, attend(): call(kernel, jax.ShapeDtypeStruct((4, 528, DH), bf) if last else (acc, to...  14.9 us
    ppermute x10, waiting for transfers between devices, send(): return lax.ppermute(value, ('blk', 'col'), perm)  14.5 us
    all_to_all x1, starting transfers between devices, body(): lax.all_to_all(packed, ('blk', 'col'), 0, 0, axis_index_groups=KV_GROUPS,...  13.3 us
    all_to_all x1, blocking collectives, body(): lax.all_to_all(part, ('blk', 'col'), 0, 0, axis_index_groups=OUT_GROUPS,...  11.4 us
  transfers between devices with their start and end apart: 11, of which 5 were waited for; matrix products, arithmetic and copies ran while one was open for 0% of the time, Pallas kernels for 14%

profile of v3, /device:TPU:6, one launch (start us, length us, event | category | flops | bytes accessed | tf_op | source)
XLA Modules:
  0.0 89.5 jit_solution(6248596493383138560)
XLA Ops:
  0.6 1.7 %pack.1 = (bf16[16,72,128]{2,1,0:T(8,128)(2,1)}, bf16[528,128]{1,0:T(8,128)(2,1)S(1)}) custom-call(s32[512]{0:T(512)} %pos_hbm.1, bf16[32,512]{1,0:T(8,128)(2,1)} %k_hbm.1, bf16[32,512]{1,0:T(8,128)(2,1)} %v_hbm.1, bf16[512,128]{1,0:T(8,128)(2,1)} %q_hbm.1), custom_call_target="tpu_custom_call" | custom-call | tf_op jit(solution)/shard_map/pack/pallas_call | solution.py:285
  2.3 13.3 %all-to-all-start = ((bf16[16,72,128]{2,1,0:T(8,128)(2,1)}), bf16[16,72,128]{2,1,0:T(8,128)(2,1)S(1)}, u32[]{:S(2)}, u32[]{:S(2)}) async-start(bf16[16,72,128]{2,1,0:T(8,128)(2,1)} %get-tuple-element.15), calls=%async_computation | async-start | bytes 589824 | tf_op jit(solution)/shard_map/all_to_all | solution.py:297
  15.6 3.4 %collective-permute-start = (bf16[528,128]{1,0:T(8,128)(2,1)S(1)}, bf16[528,128]{1,0:T(8,128)(2,1)S(1)}, u32[]{:S(2)}, u32[]{:S(2)}) collective-permute-start(bf16[528,128]{1,0:T(8,128)(2,1)S(1)} %get-tuple-element.14.refs_0_), channel_id=1, source_target_pairs={{0,1},{1,0},{2,3},{3,2},{4,5},{5,4},{6,7},{7,6},{8,9},{9,8},{10,11... | collective-permute-start | bytes 405512 | tf_op jit(solution)/shard_map/ppermute | solution.py:58
  19.0 1.9 %collective-permute-start.1 = (bf16[528,128]{1,0:T(8,128)(2,1)S(1)}, bf16[528,128]{1,0:T(8,128)(2,1)S(1)}, u32[]{:S(2)}, u32[]{:S(2)}) collective-permute-start(bf16[528,128]{1,0:T(8,128)(2,1)S(1)} %get-tuple-element.14.refs_0_), channel_id=1, source_target_pairs={{0,16},{1,17},{2,18},{3,19},{4,20},{5,21},{6,22},{7,23},{8,24},{9,... | collective-permute-start | bytes 405512 | tf_op jit(solution)/shard_map/ppermute | solution.py:58
  20.9 5.7 %collective-permute-done.refs_1_ = bf16[528,128]{1,0:T(8,128)(2,1)S(1)} collective-permute-done((bf16[528,128]{1,0:T(8,128)(2,1)S(1)}, bf16[528,128]{1,0:T(8,128)(2,1)S(1)}, u32[]{:S(2)}, u32[]{:S(2)}) %collective-permute-start) | collective-permute-done | bytes 135200 | tf_op jit(solution)/shard_map/ppermute | solution.py:58
  26.6 1.9 %collective-permute-start.2 = (bf16[528,128]{1,0:T(8,128)(2,1)S(1)}, bf16[528,128]{1,0:T(8,128)(2,1)S(1)}, u32[]{:S(2)}, u32[]{:S(2)}) collective-permute-start(bf16[528,128]{1,0:T(8,128)(2,1)S(1)} %collective-permute-done.refs_1_), channel_id=1, source_target_pairs={{0,16},{1,17},{2,18},{3,19},{4,20},{5,21},{6,22},{7,23},{8,24},{9,... | collective-permute-start | bytes 405512 | tf_op jit(solution)/shard_map/ppermute | solution.py:58
  28.9 3.5 %collective-permute-start.3 = (bf16[1040,128]{1,0:T(8,128)(2,1)S(1)}, bf16[1040,128]{1,0:T(8,128)(2,1)S(1)}, u32[]{:S(2)}, u32[]{:S(2)}) collective-permute-start(bf16[1040,128]{1,0:T(8,128)(2,1)S(1)} %prep.1.refs_4_), channel_id=1, source_target_pairs={{0,64},{1,65},{2,66},{3,67},{4,68},{5,69},{6,70},{7,71},{8,72},{9,... | collective-permute-start | bytes 798728 | tf_op jit(solution)/shard_map/ppermute | solution.py:58
  32.4 3.8 %collective-permute-start.6 = (bf16[1040,128]{1,0:T(8,128)(2,1)S(1)}, bf16[1040,128]{1,0:T(8,128)(2,1)S(1)}, u32[]{:S(2)}, u32[]{:S(2)}) collective-permute-start(bf16[1040,128]{1,0:T(8,128)(2,1)S(1)} %prep.1.refs_4_), channel_id=1, source_target_pairs={{0,448},{1,449},{2,450},{3,451},{4,452},{5,453},{6,454},{7,455},{8... | collective-permute-start | bytes 798728 | tf_op jit(solution)/shard_map/ppermute | solution.py:58
  36.2 2.5 %attend1.2 = (f32[8,144,256]{2,1,0:T(8,128)S(1)}, f32[8,8,256]{2,1,0:T(8,128)S(1)}) custom-call(bf16[528,128]{1,0:T(8,128)(2,1)S(1)} %get-tuple-element.14.refs_0_, bf16[528,128]{1,0:T(8,128)(2,1)S(1)} %collective-permute-done.refs_1_, bf16[528,128]{1,0:T(8,128)(2,1)S(1)} %collective-permute-done.1.refs_2_, ...), custom_call_target="tpu_custom_call" | custom-call | flops 2000000000 | tf_op jit(solution)/shard_map/attend1/pallas_call | solution.py:332
  38.7 2.6 %collective-permute-done.3.refs_4_ = bf16[1040,128]{1,0:T(8,128)(2,1)S(1)} collective-permute-done((bf16[1040,128]{1,0:T(8,128)(2,1)S(1)}, bf16[1040,128]{1,0:T(8,128)(2,1)S(1)}, u32[]{:S(2)}, u32[]{:S(2)}) %collective-permute-start.3) | collective-permute-done | bytes 266272 | tf_op jit(solution)/shard_map/ppermute | solution.py:58
  41.3 1.9 %collective-permute-start.4 = (bf16[1040,128]{1,0:T(8,128)(2,1)S(1)}, bf16[1040,128]{1,0:T(8,128)(2,1)S(1)}, u32[]{:S(2)}, u32[]{:S(2)}) collective-permute-start(bf16[1040,128]{1,0:T(8,128)(2,1)S(1)} %collective-permute-done.3.refs_4_), channel_id=1, source_target_pairs={{0,64},{1,65},{2,66},{3,67},{4,68},{5,69},{6,70},{7,71},{8,72},{9,... | collective-permute-start | bytes 798728 | tf_op jit(solution)/shard_map/ppermute | solution.py:58
  43.2 5.1 %collective-permute-start.7 = (bf16[1040,128]{1,0:T(8,128)(2,1)S(1)}, bf16[1040,128]{1,0:T(8,128)(2,1)S(1)}, u32[]{:S(2)}, u32[]{:S(2)}) collective-permute-start(bf16[1040,128]{1,0:T(8,128)(2,1)S(1)} %collective-permute-done.6.refs_5_), channel_id=1, source_target_pairs={{0,448},{1,449},{2,450},{3,451},{4,452},{5,453},{6,454},{7,455},{8... | collective-permute-start | bytes 798728 | tf_op jit(solution)/shard_map/ppermute | solution.py:58
  48.4 2.9 %attend2.3 = (f32[8,144,256]{2,1,0:T(8,128)S(1)}, f32[8,8,256]{2,1,0:T(8,128)S(1)}) custom-call(bf16[528,128]{1,0:T(8,128)(2,1)S(1)} %get-tuple-element.14.refs_0_, bf16[528,128]{1,0:T(8,128)(2,1)S(1)} %collective-permute-done.refs_1_, bf16[528,128]{1,0:T(8,128)(2,1)S(1)} %collective-permute-done.1.refs_2_, ...), custom_call_target="tpu_custom_call", output_to_operand_aliasing={{0}: (6, {}), {1}: (7, {})} | custom-call | flops 4000000000 | tf_op jit(solution)/shard_map/attend2/pallas_call | solution.py:332
  51.3 1.3 %collective-permute-done.4.refs_4_ = bf16[1040,128]{1,0:T(8,128)(2,1)S(1)} collective-permute-done((bf16[1040,128]{1,0:T(8,128)(2,1)S(1)}, bf16[1040,128]{1,0:T(8,128)(2,1)S(1)}, u32[]{:S(2)}, u32[]{:S(2)}) %collective-permute-start.4) | collective-permute-done | bytes 266272 | tf_op jit(solution)/shard_map/ppermute | solution.py:58
  52.6 1.9 %collective-permute-start.5 = (bf16[1040,128]{1,0:T(8,128)(2,1)S(1)}, bf16[1040,128]{1,0:T(8,128)(2,1)S(1)}, u32[]{:S(2)}, u32[]{:S(2)}) collective-permute-start(bf16[1040,128]{1,0:T(8,128)(2,1)S(1)} %collective-permute-done.4.refs_4_), channel_id=1, source_target_pairs={{0,64},{1,65},{2,66},{3,67},{4,68},{5,69},{6,70},{7,71},{8,72},{9,... | collective-permute-start | bytes 798728 | tf_op jit(solution)/shard_map/ppermute | solution.py:58
  54.5 5.1 %collective-permute-start.8 = (bf16[1040,128]{1,0:T(8,128)(2,1)S(1)}, bf16[1040,128]{1,0:T(8,128)(2,1)S(1)}, u32[]{:S(2)}, u32[]{:S(2)}) collective-permute-start(bf16[1040,128]{1,0:T(8,128)(2,1)S(1)} %collective-permute-done.7.refs_5_), channel_id=1, source_target_pairs={{0,448},{1,449},{2,450},{3,451},{4,452},{5,453},{6,454},{7,455},{8... | collective-permute-start | bytes 798728 | tf_op jit(solution)/shard_map/ppermute | solution.py:58
  59.7 3.4 %attend2.4 = (f32[8,144,256]{2,1,0:T(8,128)S(1)}, f32[8,8,256]{2,1,0:T(8,128)S(1)}) custom-call(bf16[528,128]{1,0:T(8,128)(2,1)S(1)} %get-tuple-element.14.refs_0_, bf16[528,128]{1,0:T(8,128)(2,1)S(1)} %collective-permute-done.refs_1_, bf16[528,128]{1,0:T(8,128)(2,1)S(1)} %collective-permute-done.1.refs_2_, ...), custom_call_target="tpu_custom_call", output_to_operand_aliasing={{0}: (6, {}), {1}: (7, {})} | custom-call | flops 4000000000 | tf_op jit(solution)/shard_map/attend2/pallas_call | solution.py:332
  63.1 1.2 %collective-permute-done.8.refs_5_ = bf16[1040,128]{1,0:T(8,128)(2,1)S(1)} collective-permute-done((bf16[1040,128]{1,0:T(8,128)(2,1)S(1)}, bf16[1040,128]{1,0:T(8,128)(2,1)S(1)}, u32[]{:S(2)}, u32[]{:S(2)}) %collective-permute-start.8) | collective-permute-done | bytes 266272 | tf_op jit(solution)/shard_map/ppermute | solution.py:58
  64.3 2.9 %collective-permute-start.9 = (bf16[1040,128]{1,0:T(8,128)(2,1)S(1)}, bf16[1040,128]{1,0:T(8,128)(2,1)S(1)}, u32[]{:S(2)}, u32[]{:S(2)}) collective-permute-start(bf16[1040,128]{1,0:T(8,128)(2,1)S(1)} %broadcast_select_fusion), channel_id=1, source_target_pairs={{0,64},{1,65},{2,66},{3,67},{4,68},{5,69},{6,70},{7,71},{8,72},{9,... | collective-permute-start | bytes 798728 | tf_op jit(solution)/shard_map/ppermute | solution.py:58
  67.2 3.3 %attend2.5 = (f32[8,144,256]{2,1,0:T(8,128)S(1)}, f32[8,8,256]{2,1,0:T(8,128)S(1)}) custom-call(bf16[528,128]{1,0:T(8,128)(2,1)S(1)} %get-tuple-element.14.refs_0_, bf16[528,128]{1,0:T(8,128)(2,1)S(1)} %collective-permute-done.refs_1_, bf16[528,128]{1,0:T(8,128)(2,1)S(1)} %collective-permute-done.1.refs_2_, ...), custom_call_target="tpu_custom_call", output_to_operand_aliasing={{0}: (6, {}), {1}: (7, {})} | custom-call | flops 4000000000 | tf_op jit(solution)/shard_map/attend2/pallas_call | solution.py:332
  70.5 3.8 %collective-permute-done.9.refs_4_ = bf16[1040,128]{1,0:T(8,128)(2,1)S(1)} collective-permute-done((bf16[1040,128]{1,0:T(8,128)(2,1)S(1)}, bf16[1040,128]{1,0:T(8,128)(2,1)S(1)}, u32[]{:S(2)}, u32[]{:S(2)}) %collective-permute-start.9) | collective-permute-done | bytes 266272 | tf_op jit(solution)/shard_map/ppermute | solution.py:58
  74.3 2.8 %attend1.3 = bf16[4,528,128]{2,1,0:T(8,128)(2,1)S(1)} custom-call(bf16[528,128]{1,0:T(8,128)(2,1)S(1)} %get-tuple-element.14.refs_0_, bf16[528,128]{1,0:T(8,128)(2,1)S(1)} %collective-permute-done.refs_1_, bf16[528,128]{1,0:T(8,128)(2,1)S(1)} %collective-permute-done.1.refs_2_, bf16[528,128]{1,0:T(8,128)(2,1)S(1)} %collective-permute-done.2.refs_3_, ...), custom_call_target="tpu_custom_call" | custom-call | flops 2000000000 | tf_op jit(solution)/shard_map/attend1/pallas_call | solution.py:332
  77.1 11.4 %all_to_all.10.i_ref = bf16[4,528,128]{2,1,0:T(8,128)(2,1)S(1)} all-to-all(bf16[4,528,128]{2,1,0:T(8,128)(2,1)S(1)} %attend1.3), channel_id=1, replica_groups={{0,1,16,17},{2,3,18,19},{4,5,20,21},{6,7,22,23},{8,9,24,25},{10,11,26,2..., dimensions={0} | all-to-all | bytes 1081344 | tf_op jit(solution)/shard_map/all_to_all | solution.py:347
  88.5 1.1 %merge.1 = (f32[512,128]{1,0:T(8,128)}, f32[4,128]{1,0:T(4,128)}) custom-call(bf16[4,528,128]{2,1,0:T(8,128)(2,1)S(1)} %all_to_all.10.i_ref), custom_call_target="tpu_custom_call" | custom-call | tf_op jit(solution)/shard_map/merge/pallas_call | solution.py:348
  (8 shorter events, 0.4 us)
Async XLA Ops:
  2.3 26.2 %all-to-all-start = ((bf16[16,72,128]{2,1,0:T(8,128)(2,1)}), bf16[16,72,128]{2,1,0:T(8,128)(2,1)S(1)}, u32[]{:S(2)}, u32[]{:S(2)}) async-start(bf16[16,72,128]{2,1,0:T(8,128)(2,1)} %get-tuple-element.15), calls=%async_computation | async-start | bytes 589824 | tf_op jit(solution)/shard_map/all_to_all | solution.py:297
  15.6 11.0 %collective-permute-start = (bf16[528,128]{1,0:T(8,128)(2,1)S(1)}, bf16[528,128]{1,0:T(8,128)(2,1)S(1)}, u32[]{:S(2)}, u32[]{:S(2)}) collective-permute-start(bf16[528,128]{1,0:T(8,128)(2,1)S(1)} %get-tuple-element.14.refs_0_), channel_id=1, source_target_pairs={{0,1},{1,0},{2,3},{3,2},{4,5},{5,4},{6,7},{7,6},{8,9},{9,8},{10,11... | collective-permute-start | bytes 405512 | tf_op jit(solution)/shard_map/ppermute | solution.py:58
  19.0 17.2 %collective-permute-start.1 = (bf16[528,128]{1,0:T(8,128)(2,1)S(1)}, bf16[528,128]{1,0:T(8,128)(2,1)S(1)}, u32[]{:S(2)}, u32[]{:S(2)}) collective-permute-start(bf16[528,128]{1,0:T(8,128)(2,1)S(1)} %get-tuple-element.14.refs_0_), channel_id=1, source_target_pairs={{0,16},{1,17},{2,18},{3,19},{4,20},{5,21},{6,22},{7,23},{8,24},{9,... | collective-permute-start | bytes 405512 | tf_op jit(solution)/shard_map/ppermute | solution.py:58
  26.6 9.6 %collective-permute-start.2 = (bf16[528,128]{1,0:T(8,128)(2,1)S(1)}, bf16[528,128]{1,0:T(8,128)(2,1)S(1)}, u32[]{:S(2)}, u32[]{:S(2)}) collective-permute-start(bf16[528,128]{1,0:T(8,128)(2,1)S(1)} %collective-permute-done.refs_1_), channel_id=1, source_target_pairs={{0,16},{1,17},{2,18},{3,19},{4,20},{5,21},{6,22},{7,23},{8,24},{9,... | collective-permute-start | bytes 405512 | tf_op jit(solution)/shard_map/ppermute | solution.py:58
  28.9 12.4 %collective-permute-start.3 = (bf16[1040,128]{1,0:T(8,128)(2,1)S(1)}, bf16[1040,128]{1,0:T(8,128)(2,1)S(1)}, u32[]{:S(2)}, u32[]{:S(2)}) collective-permute-start(bf16[1040,128]{1,0:T(8,128)(2,1)S(1)} %prep.1.refs_4_), channel_id=1, source_target_pairs={{0,64},{1,65},{2,66},{3,67},{4,68},{5,69},{6,70},{7,71},{8,72},{9,... | collective-permute-start | bytes 798728 | tf_op jit(solution)/shard_map/ppermute | solution.py:58
  32.4 10.9 %collective-permute-start.6 = (bf16[1040,128]{1,0:T(8,128)(2,1)S(1)}, bf16[1040,128]{1,0:T(8,128)(2,1)S(1)}, u32[]{:S(2)}, u32[]{:S(2)}) collective-permute-start(bf16[1040,128]{1,0:T(8,128)(2,1)S(1)} %prep.1.refs_4_), channel_id=1, source_target_pairs={{0,448},{1,449},{2,450},{3,451},{4,452},{5,453},{6,454},{7,455},{8... | collective-permute-start | bytes 798728 | tf_op jit(solution)/shard_map/ppermute | solution.py:58
  41.3 11.3 %collective-permute-start.4 = (bf16[1040,128]{1,0:T(8,128)(2,1)S(1)}, bf16[1040,128]{1,0:T(8,128)(2,1)S(1)}, u32[]{:S(2)}, u32[]{:S(2)}) collective-permute-start(bf16[1040,128]{1,0:T(8,128)(2,1)S(1)} %collective-permute-done.3.refs_4_), channel_id=1, source_target_pairs={{0,64},{1,65},{2,66},{3,67},{4,68},{5,69},{6,70},{7,71},{8,72},{9,... | collective-permute-start | bytes 798728 | tf_op jit(solution)/shard_map/ppermute | solution.py:58
  43.2 11.3 %collective-permute-start.7 = (bf16[1040,128]{1,0:T(8,128)(2,1)S(1)}, bf16[1040,128]{1,0:T(8,128)(2,1)S(1)}, u32[]{:S(2)}, u32[]{:S(2)}) collective-permute-start(bf16[1040,128]{1,0:T(8,128)(2,1)S(1)} %collective-permute-done.6.refs_5_), channel_id=1, source_target_pairs={{0,448},{1,449},{2,450},{3,451},{4,452},{5,453},{6,454},{7,455},{8... | collective-permute-start | bytes 798728 | tf_op jit(solution)/shard_map/ppermute | solution.py:58
  52.6 10.5 %collective-permute-start.5 = (bf16[1040,128]{1,0:T(8,128)(2,1)S(1)}, bf16[1040,128]{1,0:T(8,128)(2,1)S(1)}, u32[]{:S(2)}, u32[]{:S(2)}) collective-permute-start(bf16[1040,128]{1,0:T(8,128)(2,1)S(1)} %collective-permute-done.4.refs_4_), channel_id=1, source_target_pairs={{0,64},{1,65},{2,66},{3,67},{4,68},{5,69},{6,70},{7,71},{8,72},{9,... | collective-permute-start | bytes 798728 | tf_op jit(solution)/shard_map/ppermute | solution.py:58
  54.5 9.7 %collective-permute-start.8 = (bf16[1040,128]{1,0:T(8,128)(2,1)S(1)}, bf16[1040,128]{1,0:T(8,128)(2,1)S(1)}, u32[]{:S(2)}, u32[]{:S(2)}) collective-permute-start(bf16[1040,128]{1,0:T(8,128)(2,1)S(1)} %collective-permute-done.7.refs_5_), channel_id=1, source_target_pairs={{0,448},{1,449},{2,450},{3,451},{4,452},{5,453},{6,454},{7,455},{8... | collective-permute-start | bytes 798728 | tf_op jit(solution)/shard_map/ppermute | solution.py:58
  64.3 10.0 %collective-permute-start.9 = (bf16[1040,128]{1,0:T(8,128)(2,1)S(1)}, bf16[1040,128]{1,0:T(8,128)(2,1)S(1)}, u32[]{:S(2)}, u32[]{:S(2)}) collective-permute-start(bf16[1040,128]{1,0:T(8,128)(2,1)S(1)} %broadcast_select_fusion), channel_id=1, source_target_pairs={{0,64},{1,65},{2,66},{3,67},{4,68},{5,69},{6,70},{7,71},{8,72},{9,... | collective-permute-start | bytes 798728 | tf_op jit(solution)/shard_map/ppermute | solution.py:58

commit v4 on v2

--- a/solution.py
+++ b/solution.py
@@ -7,7 +7,7 @@
 from jax.experimental.pallas import tpu as pltpu
 from jax.sharding import PartitionSpec as P
 
-HQ = 16
+
 HK = 4
 DH = 128
 STRIPE = 128
@@ -58,7 +58,7 @@
     return lax.ppermute(value, ("blk", "col"), perm)
 
 
-def call(kernel, out, in_spaces, scratch=(), alias=None, name=None, flops=0):
+def call(kernel, out, in_spaces, scratch=(), alias=None, flops=0):
     vm = pl.BlockSpec(memory_space=VM)
     sm = pl.BlockSpec(memory_space=SM)
     return pl.pallas_call(
@@ -68,7 +68,6 @@
         out_specs=jax.tree.map(lambda _: vm, out),
         scratch_shapes=list(scratch),
         input_output_aliases=alias or {},
-        name=name,
         cost_estimate=pl.CostEstimate(flops=flops, transcendentals=0, bytes_accessed=0) if flops else None,
         compiler_params=pltpu.CompilerParams(vmem_limit_bytes=40 * 1024 * 1024),
     )
@@ -220,10 +219,10 @@
         need = jnp.int32(0)
         for n in range(nblocks):
             seen = jnp.int32(0)
-            for j in (0, 4, 6):
+            for j in (0, 2, 4, 6):
                 seen = seen + (kp[n * NST + j] <= far).astype(jnp.int32)
             need = jnp.maximum(need, seen)
-        for level, keys in ((1, 4 * SUB), (2, 6 * SUB), (3, 8 * SUB)):
+        for level, keys in ((1, 2 * SUB), (2, 4 * SUB), (3, 6 * SUB), (4, 8 * SUB)):
 
             @pl.when(need == level)
             def _(keys=keys):
@@ -292,22 +291,17 @@
             VM((32, HK * DH), bf),
             pltpu.SemaphoreType.DMA((4,)),
         ],
-        name="pack",
     )(*[pltpu.with_memory_space_constraint(a, pltpu.HBM) for a in (positions, keys, values, queries)])
     got = lax.all_to_all(packed, ("blk", "col"), 0, 0, axis_index_groups=KV_GROUPS, tiled=False)
     qz, qc = send(qo, ZPAIR), send(qo, CORE)
     qd = send(qz, CORE)
     qs = (qo, qz, qc, qd)
     own = call(
-        prep_kernel,
-        jax.ShapeDtypeStruct((ROWS, DH), bf),
-        "v",
-        scratch=[VM((BK, DH), f32), SM((NST,), jnp.int32)],
-        name="prep",
+        prep_kernel, jax.ShapeDtypeStruct((ROWS, DH), bf), "v", scratch=[VM((BK, DH), f32), SM((NST,), jnp.int32)]
     )(got)
 
     up, down = [send(own, UP)], [send(own, DOWN)]
-    for step in range(2):
+    for _ in range(2):
         up.append(send(up[-1], UP))
         down.append(send(down[-1], DOWN))
     far = send(jnp.where(core == 0, up[1], down[1]), LAST)
@@ -336,19 +330,16 @@
             scratch=scratch,
             alias=None if first or last else {4 + n: 0, 5 + n: 1},
             flops=n * 2_000_000_000,
-            name=f"attend{n}",
         )(*args)
 
     carry = attend([own], None)
     carry = attend([up[0], down[0]], carry)
     carry = attend([up[1], down[1]], carry)
-    part = attend([up[2], down[2], far], carry, last=True)
+    carry = attend([up[2]], carry)
+    part = attend([down[2], far], carry, last=True)
     parts = lax.all_to_all(part, ("blk", "col"), 0, 0, axis_index_groups=OUT_GROUPS, tiled=False)
     attended, lognorm = call(
-        merge_kernel,
-        (jax.ShapeDtypeStruct((512, DH), f32), jax.ShapeDtypeStruct((4, 128), f32)),
-        "v",
-        name="merge",
+        merge_kernel, (jax.ShapeDtypeStruct((512, DH), f32), jax.ShapeDtypeStruct((4, 128), f32)), "v"
     )(parts)
     return attended, lognorm.reshape(512, 1)
 

time: 90.3 us -> 93 us (1.030)
  waiting for transfers between devices: 12.7 us -> 16.7 us
  starting transfers between devices: 47.4 us -> 44.2 us
  Pallas kernels: 17.4 us -> 19 us
    ppermute x10, waiting for transfers between devices: 12.7 us -> 16.7 us  [send(): return lax.ppermute(value, ('blk', 'col'), perm)]
    ppermute x10, starting transfers between devices: 34.2 us -> 31 us  [send(): return lax.ppermute(value, ('blk', 'col'), perm)]
    pallas_call x4 -> x5, Pallas kernels: 14.4 us -> 15.9 us  [attend(): call(kernel, jax.ShapeDtypeStruct((4, 528, DH), bf) if last else (acc, to...]
  transfers between devices with their start and end apart: 11 -> 11, of which waited for: 5 -> 4; matrix products, arithmetic and copies ran while one was open for 0% -> 0% of each run, Pallas kernels for 11% -> 14%
where the time goes in v4:
time: 93 us; the launch traced here: 92.2 us
  starting transfers between devices  44.2 us (48%)
  Pallas kernels  19 us (20%)
  waiting for transfers between devices  16.7 us (18%)
  blocking collectives  11.4 us (12%)
    ppermute x10, starting transfers between devices, send(): return lax.ppermute(value, ('blk', 'col'), perm)  31 us
    ppermute x10, waiting for transfers between devices, send(): return lax.ppermute(value, ('blk', 'col'), perm)  16.7 us
    pallas_call x5, Pallas kernels, attend(): call(kernel, jax.ShapeDtypeStruct((4, 528, DH), bf) if last else (acc, to...  15.9 us
    all_to_all x1, starting transfers between devices, body(): lax.all_to_all(packed, ('blk', 'col'), 0, 0, axis_index_groups=KV_GROUPS,...  13.3 us
    all_to_all x1, blocking collectives, body(): lax.all_to_all(part, ('blk', 'col'), 0, 0, axis_index_groups=OUT_GROUPS,...  11.4 us
  transfers between devices with their start and end apart: 11, of which 4 were waited for; matrix products, arithmetic and copies ran while one was open for 0% of the time, Pallas kernels for 14%

profile of v4, /device:TPU:6, one launch (start us, length us, event | category | flops | bytes accessed | tf_op | source)
XLA Modules:
  0.0 92.2 jit_solution(11492035450533682941)
XLA Ops:
  0.6 1.7 %shard_map.59 = (bf16[16,72,128]{2,1,0:T(8,128)(2,1)}, bf16[528,128]{1,0:T(8,128)(2,1)S(1)}) custom-call(s32[512]{0:T(512)} %pos_hbm.1, bf16[32,512]{1,0:T(8,128)(2,1)} %k_hbm.1, bf16[32,512]{1,0:T(8,128)(2,1)} %v_hbm.1, bf16[512,128]{1,0:T(8,128)(2,1)} %q_hbm.1), custom_call_target="tpu_custom_call" | custom-call | tf_op jit(solution)/shard_map/pallas_call | solution.py:284
  2.3 13.3 %all-to-all-start = ((bf16[16,72,128]{2,1,0:T(8,128)(2,1)}), bf16[16,72,128]{2,1,0:T(8,128)(2,1)S(1)}, u32[]{:S(2)}, u32[]{:S(2)}) async-start(bf16[16,72,128]{2,1,0:T(8,128)(2,1)} %get-tuple-element.15), calls=%async_computation | async-start | bytes 589824 | tf_op jit(solution)/shard_map/all_to_all | solution.py:295
  15.6 3.4 %collective-permute-start = (bf16[528,128]{1,0:T(8,128)(2,1)S(1)}, bf16[528,128]{1,0:T(8,128)(2,1)S(1)}, u32[]{:S(2)}, u32[]{:S(2)}) collective-permute-start(bf16[528,128]{1,0:T(8,128)(2,1)S(1)} %get-tuple-element.14.refs_0_), channel_id=1, source_target_pairs={{0,1},{1,0},{2,3},{3,2},{4,5},{5,4},{6,7},{7,6},{8,9},{9,8},{10,11... | collective-permute-start | bytes 405512 | tf_op jit(solution)/shard_map/ppermute | solution.py:58
  19.0 1.9 %collective-permute-start.1 = (bf16[528,128]{1,0:T(8,128)(2,1)S(1)}, bf16[528,128]{1,0:T(8,128)(2,1)S(1)}, u32[]{:S(2)}, u32[]{:S(2)}) collective-permute-start(bf16[528,128]{1,0:T(8,128)(2,1)S(1)} %get-tuple-element.14.refs_0_), channel_id=1, source_target_pairs={{0,16},{1,17},{2,18},{3,19},{4,20},{5,21},{6,22},{7,23},{8,24},{9,... | collective-permute-start | bytes 405512 | tf_op jit(solution)/shard_map/ppermute | solution.py:58
  20.9 5.7 %collective-permute-done.refs_1_ = bf16[528,128]{1,0:T(8,128)(2,1)S(1)} collective-permute-done((bf16[528,128]{1,0:T(8,128)(2,1)S(1)}, bf16[528,128]{1,0:T(8,128)(2,1)S(1)}, u32[]{:S(2)}, u32[]{:S(2)}) %collective-permute-start) | collective-permute-done | bytes 135200 | tf_op jit(solution)/shard_map/ppermute | solution.py:58
  26.6 1.9 %collective-permute-start.2 = (bf16[528,128]{1,0:T(8,128)(2,1)S(1)}, bf16[528,128]{1,0:T(8,128)(2,1)S(1)}, u32[]{:S(2)}, u32[]{:S(2)}) collective-permute-start(bf16[528,128]{1,0:T(8,128)(2,1)S(1)} %collective-permute-done.refs_1_), channel_id=1, source_target_pairs={{0,16},{1,17},{2,18},{3,19},{4,20},{5,21},{6,22},{7,23},{8,24},{9,... | collective-permute-start | bytes 405512 | tf_op jit(solution)/shard_map/ppermute | solution.py:58
  28.5 0.3 shard_map.60.refs_4_
  28.9 5.4 %collective-permute-start.3 = (bf16[1040,128]{1,0:T(8,128)(2,1)S(1)}, bf16[1040,128]{1,0:T(8,128)(2,1)S(1)}, u32[]{:S(2)}, u32[]{:S(2)}) collective-permute-start(bf16[1040,128]{1,0:T(8,128)(2,1)S(1)} %shard_map.60.refs_4_), channel_id=1, source_target_pairs={{0,448},{1,449},{2,450},{3,451},{4,452},{5,453},{6,454},{7,455},{8... | collective-permute-start | bytes 798728 | tf_op jit(solution)/shard_map/ppermute | solution.py:58
  34.2 1.9 %collective-permute-start.6 = (bf16[1040,128]{1,0:T(8,128)(2,1)S(1)}, bf16[1040,128]{1,0:T(8,128)(2,1)S(1)}, u32[]{:S(2)}, u32[]{:S(2)}) collective-permute-start(bf16[1040,128]{1,0:T(8,128)(2,1)S(1)} %shard_map.60.refs_4_), channel_id=1, source_target_pairs={{0,64},{1,65},{2,66},{3,67},{4,68},{5,69},{6,70},{7,71},{8,72},{9,... | collective-permute-start | bytes 798728 | tf_op jit(solution)/shard_map/ppermute | solution.py:58
  36.2 2.7 %shard_map.61 = (f32[8,144,256]{2,1,0:T(8,128)S(1)}, f32[8,8,256]{2,1,0:T(8,128)S(1)}) custom-call(bf16[528,128]{1,0:T(8,128)(2,1)S(1)} %get-tuple-element.14.refs_0_, bf16[528,128]{1,0:T(8,128)(2,1)S(1)} %collective-permute-done.refs_1_, bf16[528,128]{1,0:T(8,128)(2,1)S(1)} %collective-permute-done.1.refs_2_, ...), custom_call_target="tpu_custom_call" | custom-call | flops 2000000000 | tf_op jit(solution)/shard_map/pallas_call | solution.py:326
  38.9 1.6 %collective-permute-done.3.refs_5_ = bf16[1040,128]{1,0:T(8,128)(2,1)S(1)} collective-permute-done((bf16[1040,128]{1,0:T(8,128)(2,1)S(1)}, bf16[1040,128]{1,0:T(8,128)(2,1)S(1)}, u32[]{:S(2)}, u32[]{:S(2)}) %collective-permute-start.3) | collective-permute-done | bytes 266272 | tf_op jit(solution)/shard_map/ppermute | solution.py:58
  40.5 5.6 %collective-permute-start.4 = (bf16[1040,128]{1,0:T(8,128)(2,1)S(1)}, bf16[1040,128]{1,0:T(8,128)(2,1)S(1)}, u32[]{:S(2)}, u32[]{:S(2)}) collective-permute-start(bf16[1040,128]{1,0:T(8,128)(2,1)S(1)} %collective-permute-done.3.refs_5_), channel_id=1, source_target_pairs={{0,448},{1,449},{2,450},{3,451},{4,452},{5,453},{6,454},{7,455},{8... | collective-permute-start | bytes 798728 | tf_op jit(solution)/shard_map/ppermute | solution.py:58
  46.1 1.9 %collective-permute-start.7 = (bf16[1040,128]{1,0:T(8,128)(2,1)S(1)}, bf16[1040,128]{1,0:T(8,128)(2,1)S(1)}, u32[]{:S(2)}, u32[]{:S(2)}) collective-permute-start(bf16[1040,128]{1,0:T(8,128)(2,1)S(1)} %collective-permute-done.6.refs_4_), channel_id=1, source_target_pairs={{0,64},{1,65},{2,66},{3,67},{4,68},{5,69},{6,70},{7,71},{8,72},{9,... | collective-permute-start | bytes 798728 | tf_op jit(solution)/shard_map/ppermute | solution.py:58
  48.1 3.5 %shard_map.62 = (f32[8,144,256]{2,1,0:T(8,128)S(1)}, f32[8,8,256]{2,1,0:T(8,128)S(1)}) custom-call(bf16[528,128]{1,0:T(8,128)(2,1)S(1)} %get-tuple-element.14.refs_0_, bf16[528,128]{1,0:T(8,128)(2,1)S(1)} %collective-permute-done.refs_1_, bf16[528,128]{1,0:T(8,128)(2,1)S(1)} %collective-permute-done.1.refs_2_, ...), custom_call_target="tpu_custom_call", output_to_operand_aliasing={{0}: (6, {}), {1}: (7, {})} | custom-call | flops 4000000000 | tf_op jit(solution)/shard_map/pallas_call | solution.py:326
  51.6 5.3 %collective-permute-done.7.refs_4_ = bf16[1040,128]{1,0:T(8,128)(2,1)S(1)} collective-permute-done((bf16[1040,128]{1,0:T(8,128)(2,1)S(1)}, bf16[1040,128]{1,0:T(8,128)(2,1)S(1)}, u32[]{:S(2)}, u32[]{:S(2)}) %collective-permute-start.7) | collective-permute-done | bytes 266272 | tf_op jit(solution)/shard_map/ppermute | solution.py:58
  56.9 1.9 %collective-permute-start.8 = (bf16[1040,128]{1,0:T(8,128)(2,1)S(1)}, bf16[1040,128]{1,0:T(8,128)(2,1)S(1)}, u32[]{:S(2)}, u32[]{:S(2)}) collective-permute-start(bf16[1040,128]{1,0:T(8,128)(2,1)S(1)} %broadcast_select_fusion), channel_id=1, source_target_pairs={{0,128},{1,129},{2,130},{3,131},{4,132},{5,133},{6,134},{7,135},{8... | collective-permute-start | bytes 798728 | tf_op jit(solution)/shard_map/ppermute | solution.py:58
  58.9 2.1 %collective-permute-start.9 = (bf16[1040,128]{1,0:T(8,128)(2,1)S(1)}, bf16[1040,128]{1,0:T(8,128)(2,1)S(1)}, u32[]{:S(2)}, u32[]{:S(2)}) collective-permute-start(bf16[1040,128]{1,0:T(8,128)(2,1)S(1)} %collective-permute-done.7.refs_4_), channel_id=1, source_target_pairs={{0,64},{1,65},{2,66},{3,67},{4,68},{5,69},{6,70},{7,71},{8,72},{9,... | collective-permute-start | bytes 798728 | tf_op jit(solution)/shard_map/ppermute | solution.py:58
  61.0 4.9 %collective-permute-start.5 = (bf16[1040,128]{1,0:T(8,128)(2,1)S(1)}, bf16[1040,128]{1,0:T(8,128)(2,1)S(1)}, u32[]{:S(2)}, u32[]{:S(2)}) collective-permute-start(bf16[1040,128]{1,0:T(8,128)(2,1)S(1)} %collective-permute-done.4.refs_5_), channel_id=1, source_target_pairs={{0,448},{1,449},{2,450},{3,451},{4,452},{5,453},{6,454},{7,455},{8... | collective-permute-start | bytes 798728 | tf_op jit(solution)/shard_map/ppermute | solution.py:58
  65.9 3.5 %shard_map.63 = (f32[8,144,256]{2,1,0:T(8,128)S(1)}, f32[8,8,256]{2,1,0:T(8,128)S(1)}) custom-call(bf16[528,128]{1,0:T(8,128)(2,1)S(1)} %get-tuple-element.14.refs_0_, bf16[528,128]{1,0:T(8,128)(2,1)S(1)} %collective-permute-done.refs_1_, bf16[528,128]{1,0:T(8,128)(2,1)S(1)} %collective-permute-done.1.refs_2_, ...), custom_call_target="tpu_custom_call", output_to_operand_aliasing={{0}: (6, {}), {1}: (7, {})} | custom-call | flops 4000000000 | tf_op jit(solution)/shard_map/pallas_call | solution.py:326
  69.5 4.1 %collective-permute-done.9.refs_4_ = bf16[1040,128]{1,0:T(8,128)(2,1)S(1)} collective-permute-done((bf16[1040,128]{1,0:T(8,128)(2,1)S(1)}, bf16[1040,128]{1,0:T(8,128)(2,1)S(1)}, u32[]{:S(2)}, u32[]{:S(2)}) %collective-permute-start.9) | collective-permute-done | bytes 266272 | tf_op jit(solution)/shard_map/ppermute | solution.py:58
  73.5 2.6 %shard_map.64 = (f32[8,144,256]{2,1,0:T(8,128)S(1)}, f32[8,8,256]{2,1,0:T(8,128)S(1)}) custom-call(bf16[528,128]{1,0:T(8,128)(2,1)S(1)} %get-tuple-element.14.refs_0_, bf16[528,128]{1,0:T(8,128)(2,1)S(1)} %collective-permute-done.refs_1_, bf16[528,128]{1,0:T(8,128)(2,1)S(1)} %collective-permute-done.1.refs_2_, ...), custom_call_target="tpu_custom_call", output_to_operand_aliasing={{0}: (5, {}), {1}: (6, {})} | custom-call | flops 2000000000 | tf_op jit(solution)/shard_map/pallas_call | solution.py:326
  76.1 3.6 %shard_map.65 = bf16[4,528,128]{2,1,0:T(8,128)(2,1)S(1)} custom-call(bf16[528,128]{1,0:T(8,128)(2,1)S(1)} %get-tuple-element.14.refs_0_, bf16[528,128]{1,0:T(8,128)(2,1)S(1)} %collective-permute-done.refs_1_, bf16[528,128]{1,0:T(8,128)(2,1)S(1)} %collective-permute-done.1.refs_2_, bf16[528,128]{1,0:T(8,128)(2,1)S(1)} %collective-permute-done.2.refs_3_, ...), custom_call_target="tpu_custom_call" | custom-call | flops 4000000000 | tf_op jit(solution)/shard_map/pallas_call | solution.py:326
  79.8 11.4 %all_to_all.10.i_ref = bf16[4,528,128]{2,1,0:T(8,128)(2,1)S(1)} all-to-all(bf16[4,528,128]{2,1,0:T(8,128)(2,1)S(1)} %shard_map.65), channel_id=1, replica_groups={{0,1,16,17},{2,3,18,19},{4,5,20,21},{6,7,22,23},{8,9,24,25},{10,11,26,2..., dimensions={0} | all-to-all | bytes 1081344 | tf_op jit(solution)/shard_map/all_to_all | solution.py:340
  91.1 1.1 %shard_map.66 = (f32[512,128]{1,0:T(8,128)}, f32[4,128]{1,0:T(4,128)}) custom-call(bf16[4,528,128]{2,1,0:T(8,128)(2,1)S(1)} %all_to_all.10.i_ref), custom_call_target="tpu_custom_call" | custom-call | tf_op jit(solution)/shard_map/pallas_call | solution.py:341
  (8 shorter events, 0.0 us)
Async XLA Ops:
  2.3 26.2 %all-to-all-start = ((bf16[16,72,128]{2,1,0:T(8,128)(2,1)}), bf16[16,72,128]{2,1,0:T(8,128)(2,1)S(1)}, u32[]{:S(2)}, u32[]{:S(2)}) async-start(bf16[16,72,128]{2,1,0:T(8,128)(2,1)} %get-tuple-element.15), calls=%async_computation | async-start | bytes 589824 | tf_op jit(solution)/shard_map/all_to_all | solution.py:295
  15.6 11.0 %collective-permute-start = (bf16[528,128]{1,0:T(8,128)(2,1)S(1)}, bf16[528,128]{1,0:T(8,128)(2,1)S(1)}, u32[]{:S(2)}, u32[]{:S(2)}) collective-permute-start(bf16[528,128]{1,0:T(8,128)(2,1)S(1)} %get-tuple-element.14.refs_0_), channel_id=1, source_target_pairs={{0,1},{1,0},{2,3},{3,2},{4,5},{5,4},{6,7},{7,6},{8,9},{9,8},{10,11... | collective-permute-start | bytes 405512 | tf_op jit(solution)/shard_map/ppermute | solution.py:58
  19.0 17.2 %collective-permute-start.1 = (bf16[528,128]{1,0:T(8,128)(2,1)S(1)}, bf16[528,128]{1,0:T(8,128)(2,1)S(1)}, u32[]{:S(2)}, u32[]{:S(2)}) collective-permute-start(bf16[528,128]{1,0:T(8,128)(2,1)S(1)} %get-tuple-element.14.refs_0_), channel_id=1, source_target_pairs={{0,16},{1,17},{2,18},{3,19},{4,20},{5,21},{6,22},{7,23},{8,24},{9,... | collective-permute-start | bytes 405512 | tf_op jit(solution)/shard_map/ppermute | solution.py:58
  26.6 9.6 %collective-permute-start.2 = (bf16[528,128]{1,0:T(8,128)(2,1)S(1)}, bf16[528,128]{1,0:T(8,128)(2,1)S(1)}, u32[]{:S(2)}, u32[]{:S(2)}) collective-permute-start(bf16[528,128]{1,0:T(8,128)(2,1)S(1)} %collective-permute-done.refs_1_), channel_id=1, source_target_pairs={{0,16},{1,17},{2,18},{3,19},{4,20},{5,21},{6,22},{7,23},{8,24},{9,... | collective-permute-start | bytes 405512 | tf_op jit(solution)/shard_map/ppermute | solution.py:58
  28.9 11.7 %collective-permute-start.3 = (bf16[1040,128]{1,0:T(8,128)(2,1)S(1)}, bf16[1040,128]{1,0:T(8,128)(2,1)S(1)}, u32[]{:S(2)}, u32[]{:S(2)}) collective-permute-start(bf16[1040,128]{1,0:T(8,128)(2,1)S(1)} %shard_map.60.refs_4_), channel_id=1, source_target_pairs={{0,448},{1,449},{2,450},{3,451},{4,452},{5,453},{6,454},{7,455},{8... | collective-permute-start | bytes 798728 | tf_op jit(solution)/shard_map/ppermute | solution.py:58
  34.2 11.9 %collective-permute-start.6 = (bf16[1040,128]{1,0:T(8,128)(2,1)S(1)}, bf16[1040,128]{1,0:T(8,128)(2,1)S(1)}, u32[]{:S(2)}, u32[]{:S(2)}) collective-permute-start(bf16[1040,128]{1,0:T(8,128)(2,1)S(1)} %shard_map.60.refs_4_), channel_id=1, source_target_pairs={{0,64},{1,65},{2,66},{3,67},{4,68},{5,69},{6,70},{7,71},{8,72},{9,... | collective-permute-start | bytes 798728 | tf_op jit(solution)/shard_map/ppermute | solution.py:58
  40.5 11.0 %collective-permute-start.4 = (bf16[1040,128]{1,0:T(8,128)(2,1)S(1)}, bf16[1040,128]{1,0:T(8,128)(2,1)S(1)}, u32[]{:S(2)}, u32[]{:S(2)}) collective-permute-start(bf16[1040,128]{1,0:T(8,128)(2,1)S(1)} %collective-permute-done.3.refs_5_), channel_id=1, source_target_pairs={{0,448},{1,449},{2,450},{3,451},{4,452},{5,453},{6,454},{7,455},{8... | collective-permute-start | bytes 798728 | tf_op jit(solution)/shard_map/ppermute | solution.py:58
  46.1 10.8 %collective-permute-start.7 = (bf16[1040,128]{1,0:T(8,128)(2,1)S(1)}, bf16[1040,128]{1,0:T(8,128)(2,1)S(1)}, u32[]{:S(2)}, u32[]{:S(2)}) collective-permute-start(bf16[1040,128]{1,0:T(8,128)(2,1)S(1)} %collective-permute-done.6.refs_4_), channel_id=1, source_target_pairs={{0,64},{1,65},{2,66},{3,67},{4,68},{5,69},{6,70},{7,71},{8,72},{9,... | collective-permute-start | bytes 798728 | tf_op jit(solution)/shard_map/ppermute | solution.py:58
  56.9 19.2 %collective-permute-start.8 = (bf16[1040,128]{1,0:T(8,128)(2,1)S(1)}, bf16[1040,128]{1,0:T(8,128)(2,1)S(1)}, u32[]{:S(2)}, u32[]{:S(2)}) collective-permute-start(bf16[1040,128]{1,0:T(8,128)(2,1)S(1)} %broadcast_select_fusion), channel_id=1, source_target_pairs={{0,128},{1,129},{2,130},{3,131},{4,132},{5,133},{6,134},{7,135},{8... | collective-permute-start | bytes 798728 | tf_op jit(solution)/shard_map/ppermute | solution.py:58
  58.9 14.7 %collective-permute-start.9 = (bf16[1040,128]{1,0:T(8,128)(2,1)S(1)}, bf16[1040,128]{1,0:T(8,128)(2,1)S(1)}, u32[]{:S(2)}, u32[]{:S(2)}) collective-permute-start(bf16[1040,128]{1,0:T(8,128)(2,1)S(1)} %collective-permute-done.7.refs_4_), channel_id=1, source_target_pairs={{0,64},{1,65},{2,66},{3,67},{4,68},{5,69},{6,70},{7,71},{8,72},{9,... | collective-permute-start | bytes 798728 | tf_op jit(solution)/shard_map/ppermute | solution.py:58
  61.0 15.1 %collective-permute-start.5 = (bf16[1040,128]{1,0:T(8,128)(2,1)S(1)}, bf16[1040,128]{1,0:T(8,128)(2,1)S(1)}, u32[]{:S(2)}, u32[]{:S(2)}) collective-permute-start(bf16[1040,128]{1,0:T(8,128)(2,1)S(1)} %collective-permute-done.4.refs_5_), channel_id=1, source_target_pairs={{0,448},{1,449},{2,450},{3,451},{4,452},{5,453},{6,454},{7,455},{8... | collective-permute-start | bytes 798728 | tf_op jit(solution)/shard_map/ppermute | solution.py:58

commit v5 on v4

--- a/solution.py
+++ b/solution.py
@@ -300,7 +300,8 @@
         prep_kernel, jax.ShapeDtypeStruct((ROWS, DH), bf), "v", scratch=[VM((BK, DH), f32), SM((NST,), jnp.int32)]
     )(got)
 
-    up, down = [send(own, UP)], [send(own, DOWN)]
+    up = [send(own, UP)]
+    down = [send(own, DOWN)]
     for _ in range(2):
         up.append(send(up[-1], UP))
         down.append(send(down[-1], DOWN))
@@ -335,8 +336,8 @@
     carry = attend([own], None)
     carry = attend([up[0], down[0]], carry)
     carry = attend([up[1], down[1]], carry)
-    carry = attend([up[2]], carry)
-    part = attend([down[2], far], carry, last=True)
+    carry = attend([up[2], down[2]], carry)
+    part = attend([far], carry, last=True)
     parts = lax.all_to_all(part, ("blk", "col"), 0, 0, axis_index_groups=OUT_GROUPS, tiled=False)
     attended, lognorm = call(
         merge_kernel, (jax.ShapeDtypeStruct((512, DH), f32), jax.ShapeDtypeStruct((4, 128), f32)), "v"

time: 93 us -> 92 us (0.989)
  waiting for transfers between devices: 16.7 us -> 12.6 us
  starting transfers between devices: 44.2 us -> 47.4 us
    ppermute x10, waiting for transfers between devices: 16.7 us -> 12.6 us  [send(): return lax.ppermute(value, ('blk', 'col'), perm)]
    ppermute x10, starting transfers between devices: 31 us -> 34.2 us  [send(): return lax.ppermute(value, ('blk', 'col'), perm)]
  transfers between devices with their start and end apart: 11 -> 11, of which waited for: 4 -> 5; matrix products, arithmetic and copies ran while one was open for 0% -> 0% of each run, Pallas kernels for 14% -> 14%
where the time goes in v5:
time: 92 us; the launch traced here: 91.1 us
  starting transfers between devices  47.4 us (52%)
  Pallas kernels  18.8 us (20%)
  waiting for transfers between devices  12.6 us (14%)
  blocking collectives  11.4 us (12%)
    ppermute x10, starting transfers between devices, send(): return lax.ppermute(value, ('blk', 'col'), perm)  34.2 us
    pallas_call x5, Pallas kernels, attend(): call(kernel, jax.ShapeDtypeStruct((4, 528, DH), bf) if last else (acc, to...  15.7 us
    all_to_all x1, starting transfers between devices, body(): lax.all_to_all(packed, ('blk', 'col'), 0, 0, axis_index_groups=KV_GROUPS,...  13.3 us
    ppermute x10, waiting for transfers between devices, send(): return lax.ppermute(value, ('blk', 'col'), perm)  12.6 us
    all_to_all x1, blocking collectives, body(): lax.all_to_all(part, ('blk', 'col'), 0, 0, axis_index_groups=OUT_GROUPS,...  11.4 us
  transfers between devices with their start and end apart: 11, of which 5 were waited for; matrix products, arithmetic and copies ran while one was open for 0% of the time, Pallas kernels for 14%

profile of v5, /device:TPU:6, one launch (start us, length us, event | category | flops | bytes accessed | tf_op | source)
XLA Modules:
  0.0 91.1 jit_solution(18043407634095662810)
XLA Ops:
  0.6 1.7 %shard_map.59 = (bf16[16,72,128]{2,1,0:T(8,128)(2,1)}, bf16[528,128]{1,0:T(8,128)(2,1)S(1)}) custom-call(s32[512]{0:T(512)} %pos_hbm.1, bf16[32,512]{1,0:T(8,128)(2,1)} %k_hbm.1, bf16[32,512]{1,0:T(8,128)(2,1)} %v_hbm.1, bf16[512,128]{1,0:T(8,128)(2,1)} %q_hbm.1), custom_call_target="tpu_custom_call" | custom-call | tf_op jit(solution)/shard_map/pallas_call | solution.py:284
  2.3 13.3 %all-to-all-start = ((bf16[16,72,128]{2,1,0:T(8,128)(2,1)}), bf16[16,72,128]{2,1,0:T(8,128)(2,1)S(1)}, u32[]{:S(2)}, u32[]{:S(2)}) async-start(bf16[16,72,128]{2,1,0:T(8,128)(2,1)} %get-tuple-element.15), calls=%async_computation | async-start | bytes 589824 | tf_op jit(solution)/shard_map/all_to_all | solution.py:295
  15.6 3.4 %collective-permute-start = (bf16[528,128]{1,0:T(8,128)(2,1)S(1)}, bf16[528,128]{1,0:T(8,128)(2,1)S(1)}, u32[]{:S(2)}, u32[]{:S(2)}) collective-permute-start(bf16[528,128]{1,0:T(8,128)(2,1)S(1)} %get-tuple-element.14.refs_0_), channel_id=1, source_target_pairs={{0,1},{1,0},{2,3},{3,2},{4,5},{5,4},{6,7},{7,6},{8,9},{9,8},{10,11... | collective-permute-start | bytes 405512 | tf_op jit(solution)/shard_map/ppermute | solution.py:58
  19.0 1.9 %collective-permute-start.1 = (bf16[528,128]{1,0:T(8,128)(2,1)S(1)}, bf16[528,128]{1,0:T(8,128)(2,1)S(1)}, u32[]{:S(2)}, u32[]{:S(2)}) collective-permute-start(bf16[528,128]{1,0:T(8,128)(2,1)S(1)} %get-tuple-element.14.refs_0_), channel_id=1, source_target_pairs={{0,16},{1,17},{2,18},{3,19},{4,20},{5,21},{6,22},{7,23},{8,24},{9,... | collective-permute-start | bytes 405512 | tf_op jit(solution)/shard_map/ppermute | solution.py:58
  20.9 5.7 %collective-permute-done.refs_1_ = bf16[528,128]{1,0:T(8,128)(2,1)S(1)} collective-permute-done((bf16[528,128]{1,0:T(8,128)(2,1)S(1)}, bf16[528,128]{1,0:T(8,128)(2,1)S(1)}, u32[]{:S(2)}, u32[]{:S(2)}) %collective-permute-start) | collective-permute-done | bytes 135200 | tf_op jit(solution)/shard_map/ppermute | solution.py:58
  26.6 1.9 %collective-permute-start.2 = (bf16[528,128]{1,0:T(8,128)(2,1)S(1)}, bf16[528,128]{1,0:T(8,128)(2,1)S(1)}, u32[]{:S(2)}, u32[]{:S(2)}) collective-permute-start(bf16[528,128]{1,0:T(8,128)(2,1)S(1)} %collective-permute-done.refs_1_), channel_id=1, source_target_pairs={{0,16},{1,17},{2,18},{3,19},{4,20},{5,21},{6,22},{7,23},{8,24},{9,... | collective-permute-start | bytes 405512 | tf_op jit(solution)/shard_map/ppermute | solution.py:58
  28.9 3.5 %collective-permute-start.3 = (bf16[1040,128]{1,0:T(8,128)(2,1)S(1)}, bf16[1040,128]{1,0:T(8,128)(2,1)S(1)}, u32[]{:S(2)}, u32[]{:S(2)}) collective-permute-start(bf16[1040,128]{1,0:T(8,128)(2,1)S(1)} %shard_map.60.refs_4_), channel_id=1, source_target_pairs={{0,64},{1,65},{2,66},{3,67},{4,68},{5,69},{6,70},{7,71},{8,72},{9,... | collective-permute-start | bytes 798728 | tf_op jit(solution)/shard_map/ppermute | solution.py:58
  32.4 3.8 %collective-permute-start.5 = (bf16[1040,128]{1,0:T(8,128)(2,1)S(1)}, bf16[1040,128]{1,0:T(8,128)(2,1)S(1)}, u32[]{:S(2)}, u32[]{:S(2)}) collective-permute-start(bf16[1040,128]{1,0:T(8,128)(2,1)S(1)} %shard_map.60.refs_4_), channel_id=1, source_target_pairs={{0,448},{1,449},{2,450},{3,451},{4,452},{5,453},{6,454},{7,455},{8... | collective-permute-start | bytes 798728 | tf_op jit(solution)/shard_map/ppermute | solution.py:58
  36.2 2.7 %shard_map.61 = (f32[8,144,256]{2,1,0:T(8,128)S(1)}, f32[8,8,256]{2,1,0:T(8,128)S(1)}) custom-call(bf16[528,128]{1,0:T(8,128)(2,1)S(1)} %get-tuple-element.14.refs_0_, bf16[528,128]{1,0:T(8,128)(2,1)S(1)} %collective-permute-done.refs_1_, bf16[528,128]{1,0:T(8,128)(2,1)S(1)} %collective-permute-done.1.refs_2_, ...), custom_call_target="tpu_custom_call" | custom-call | flops 2000000000 | tf_op jit(solution)/shard_map/pallas_call | solution.py:327
  38.9 2.4 %collective-permute-done.3.refs_4_ = bf16[1040,128]{1,0:T(8,128)(2,1)S(1)} collective-permute-done((bf16[1040,128]{1,0:T(8,128)(2,1)S(1)}, bf16[1040,128]{1,0:T(8,128)(2,1)S(1)}, u32[]{:S(2)}, u32[]{:S(2)}) %collective-permute-start.3) | collective-permute-done | bytes 266272 | tf_op jit(solution)/shard_map/ppermute | solution.py:58
  41.3 1.9 %collective-permute-start.4 = (bf16[1040,128]{1,0:T(8,128)(2,1)S(1)}, bf16[1040,128]{1,0:T(8,128)(2,1)S(1)}, u32[]{:S(2)}, u32[]{:S(2)}) collective-permute-start(bf16[1040,128]{1,0:T(8,128)(2,1)S(1)} %collective-permute-done.3.refs_4_), channel_id=1, source_target_pairs={{0,64},{1,65},{2,66},{3,67},{4,68},{5,69},{6,70},{7,71},{8,72},{9,... | collective-permute-start | bytes 798728 | tf_op jit(solution)/shard_map/ppermute | solution.py:58
  43.2 5.1 %collective-permute-start.6 = (bf16[1040,128]{1,0:T(8,128)(2,1)S(1)}, bf16[1040,128]{1,0:T(8,128)(2,1)S(1)}, u32[]{:S(2)}, u32[]{:S(2)}) collective-permute-start(bf16[1040,128]{1,0:T(8,128)(2,1)S(1)} %collective-permute-done.5.refs_5_), channel_id=1, source_target_pairs={{0,448},{1,449},{2,450},{3,451},{4,452},{5,453},{6,454},{7,455},{8... | collective-permute-start | bytes 798728 | tf_op jit(solution)/shard_map/ppermute | solution.py:58
  48.4 3.5 %shard_map.62 = (f32[8,144,256]{2,1,0:T(8,128)S(1)}, f32[8,8,256]{2,1,0:T(8,128)S(1)}) custom-call(bf16[528,128]{1,0:T(8,128)(2,1)S(1)} %get-tuple-element.14.refs_0_, bf16[528,128]{1,0:T(8,128)(2,1)S(1)} %collective-permute-done.refs_1_, bf16[528,128]{1,0:T(8,128)(2,1)S(1)} %collective-permute-done.1.refs_2_, ...), custom_call_target="tpu_custom_call", output_to_operand_aliasing={{0}: (6, {}), {1}: (7, {})} | custom-call | flops 4000000000 | tf_op jit(solution)/shard_map/pallas_call | solution.py:327
  51.9 0.7 collective-permute-done.4.refs_4_
  52.6 1.2 %collective-permute-done.6.refs_5_ = bf16[1040,128]{1,0:T(8,128)(2,1)S(1)} collective-permute-done((bf16[1040,128]{1,0:T(8,128)(2,1)S(1)}, bf16[1040,128]{1,0:T(8,128)(2,1)S(1)}, u32[]{:S(2)}, u32[]{:S(2)}) %collective-permute-start.6) | collective-permute-done | bytes 266272 | tf_op jit(solution)/shard_map/ppermute | solution.py:58
  53.8 5.6 %collective-permute-start.7 = (bf16[1040,128]{1,0:T(8,128)(2,1)S(1)}, bf16[1040,128]{1,0:T(8,128)(2,1)S(1)}, u32[]{:S(2)}, u32[]{:S(2)}) collective-permute-start(bf16[1040,128]{1,0:T(8,128)(2,1)S(1)} %broadcast_select_fusion), channel_id=1, source_target_pairs={{0,128},{1,129},{2,130},{3,131},{4,132},{5,133},{6,134},{7,135},{8... | collective-permute-start | bytes 798728 | tf_op jit(solution)/shard_map/ppermute | solution.py:58
  59.4 4.9 %collective-permute-start.8 = (bf16[1040,128]{1,0:T(8,128)(2,1)S(1)}, bf16[1040,128]{1,0:T(8,128)(2,1)S(1)}, u32[]{:S(2)}, u32[]{:S(2)}) collective-permute-start(bf16[1040,128]{1,0:T(8,128)(2,1)S(1)} %collective-permute-done.4.refs_4_), channel_id=1, source_target_pairs={{0,64},{1,65},{2,66},{3,67},{4,68},{5,69},{6,70},{7,71},{8,72},{9,... | collective-permute-start | bytes 798728 | tf_op jit(solution)/shard_map/ppermute | solution.py:58
  64.3 2.2 %collective-permute-start.9 = (bf16[1040,128]{1,0:T(8,128)(2,1)S(1)}, bf16[1040,128]{1,0:T(8,128)(2,1)S(1)}, u32[]{:S(2)}, u32[]{:S(2)}) collective-permute-start(bf16[1040,128]{1,0:T(8,128)(2,1)S(1)} %collective-permute-done.6.refs_5_), channel_id=1, source_target_pairs={{0,448},{1,449},{2,450},{3,451},{4,452},{5,453},{6,454},{7,455},{8... | collective-permute-start | bytes 798728 | tf_op jit(solution)/shard_map/ppermute | solution.py:58
  66.5 3.5 %shard_map.63 = (f32[8,144,256]{2,1,0:T(8,128)S(1)}, f32[8,8,256]{2,1,0:T(8,128)S(1)}) custom-call(bf16[528,128]{1,0:T(8,128)(2,1)S(1)} %get-tuple-element.14.refs_0_, bf16[528,128]{1,0:T(8,128)(2,1)S(1)} %collective-permute-done.refs_1_, bf16[528,128]{1,0:T(8,128)(2,1)S(1)} %collective-permute-done.1.refs_2_, ...), custom_call_target="tpu_custom_call", output_to_operand_aliasing={{0}: (6, {}), {1}: (7, {})} | custom-call | flops 4000000000 | tf_op jit(solution)/shard_map/pallas_call | solution.py:327
  70.0 2.6 %collective-permute-done.8.refs_4_ = bf16[1040,128]{1,0:T(8,128)(2,1)S(1)} collective-permute-done((bf16[1040,128]{1,0:T(8,128)(2,1)S(1)}, bf16[1040,128]{1,0:T(8,128)(2,1)S(1)}, u32[]{:S(2)}, u32[]{:S(2)}) %collective-permute-start.8) | collective-permute-done | bytes 266272 | tf_op jit(solution)/shard_map/ppermute | solution.py:58
  72.6 3.0 %shard_map.64 = (f32[8,144,256]{2,1,0:T(8,128)S(1)}, f32[8,8,256]{2,1,0:T(8,128)S(1)}) custom-call(bf16[528,128]{1,0:T(8,128)(2,1)S(1)} %get-tuple-element.14.refs_0_, bf16[528,128]{1,0:T(8,128)(2,1)S(1)} %collective-permute-done.refs_1_, bf16[528,128]{1,0:T(8,128)(2,1)S(1)} %collective-permute-done.1.refs_2_, ...), custom_call_target="tpu_custom_call", output_to_operand_aliasing={{0}: (6, {}), {1}: (7, {})} | custom-call | flops 4000000000 | tf_op jit(solution)/shard_map/pallas_call | solution.py:327
  75.6 3.0 %shard_map.65 = bf16[4,528,128]{2,1,0:T(8,128)(2,1)S(1)} custom-call(bf16[528,128]{1,0:T(8,128)(2,1)S(1)} %get-tuple-element.14.refs_0_, bf16[528,128]{1,0:T(8,128)(2,1)S(1)} %collective-permute-done.refs_1_, bf16[528,128]{1,0:T(8,128)(2,1)S(1)} %collective-permute-done.1.refs_2_, bf16[528,128]{1,0:T(8,128)(2,1)S(1)} %collective-permute-done.2.refs_3_, ...), custom_call_target="tpu_custom_call" | custom-call | flops 2000000000 | tf_op jit(solution)/shard_map/pallas_call | solution.py:327
  78.6 11.4 %all_to_all.10.i_ref = bf16[4,528,128]{2,1,0:T(8,128)(2,1)S(1)} all-to-all(bf16[4,528,128]{2,1,0:T(8,128)(2,1)S(1)} %shard_map.65), channel_id=1, replica_groups={{0,1,16,17},{2,3,18,19},{4,5,20,21},{6,7,22,23},{8,9,24,25},{10,11,26,2..., dimensions={0} | all-to-all | bytes 1081344 | tf_op jit(solution)/shard_map/all_to_all | solution.py:341
  90.0 1.1 %shard_map.66 = (f32[512,128]{1,0:T(8,128)}, f32[4,128]{1,0:T(4,128)}) custom-call(bf16[4,528,128]{2,1,0:T(8,128)(2,1)S(1)} %all_to_all.10.i_ref), custom_call_target="tpu_custom_call" | custom-call | tf_op jit(solution)/shard_map/pallas_call | solution.py:342
  (8 shorter events, 0.4 us)
Async XLA Ops:
  2.3 26.2 %all-to-all-start = ((bf16[16,72,128]{2,1,0:T(8,128)(2,1)}), bf16[16,72,128]{2,1,0:T(8,128)(2,1)S(1)}, u32[]{:S(2)}, u32[]{:S(2)}) async-start(bf16[16,72,128]{2,1,0:T(8,128)(2,1)} %get-tuple-element.15), calls=%async_computation | async-start | bytes 589824 | tf_op jit(solution)/shard_map/all_to_all | solution.py:295
  15.6 11.0 %collective-permute-start = (bf16[528,128]{1,0:T(8,128)(2,1)S(1)}, bf16[528,128]{1,0:T(8,128)(2,1)S(1)}, u32[]{:S(2)}, u32[]{:S(2)}) collective-permute-start(bf16[528,128]{1,0:T(8,128)(2,1)S(1)} %get-tuple-element.14.refs_0_), channel_id=1, source_target_pairs={{0,1},{1,0},{2,3},{3,2},{4,5},{5,4},{6,7},{7,6},{8,9},{9,8},{10,11... | collective-permute-start | bytes 405512 | tf_op jit(solution)/shard_map/ppermute | solution.py:58
  19.0 17.2 %collective-permute-start.1 = (bf16[528,128]{1,0:T(8,128)(2,1)S(1)}, bf16[528,128]{1,0:T(8,128)(2,1)S(1)}, u32[]{:S(2)}, u32[]{:S(2)}) collective-permute-start(bf16[528,128]{1,0:T(8,128)(2,1)S(1)} %get-tuple-element.14.refs_0_), channel_id=1, source_target_pairs={{0,16},{1,17},{2,18},{3,19},{4,20},{5,21},{6,22},{7,23},{8,24},{9,... | collective-permute-start | bytes 405512 | tf_op jit(solution)/shard_map/ppermute | solution.py:58
  26.6 9.6 %collective-permute-start.2 = (bf16[528,128]{1,0:T(8,128)(2,1)S(1)}, bf16[528,128]{1,0:T(8,128)(2,1)S(1)}, u32[]{:S(2)}, u32[]{:S(2)}) collective-permute-start(bf16[528,128]{1,0:T(8,128)(2,1)S(1)} %collective-permute-done.refs_1_), channel_id=1, source_target_pairs={{0,16},{1,17},{2,18},{3,19},{4,20},{5,21},{6,22},{7,23},{8,24},{9,... | collective-permute-start | bytes 405512 | tf_op jit(solution)/shard_map/ppermute | solution.py:58
  28.9 12.4 %collective-permute-start.3 = (bf16[1040,128]{1,0:T(8,128)(2,1)S(1)}, bf16[1040,128]{1,0:T(8,128)(2,1)S(1)}, u32[]{:S(2)}, u32[]{:S(2)}) collective-permute-start(bf16[1040,128]{1,0:T(8,128)(2,1)S(1)} %shard_map.60.refs_4_), channel_id=1, source_target_pairs={{0,64},{1,65},{2,66},{3,67},{4,68},{5,69},{6,70},{7,71},{8,72},{9,... | collective-permute-start | bytes 798728 | tf_op jit(solution)/shard_map/ppermute | solution.py:58
  32.4 10.9 %collective-permute-start.5 = (bf16[1040,128]{1,0:T(8,128)(2,1)S(1)}, bf16[1040,128]{1,0:T(8,128)(2,1)S(1)}, u32[]{:S(2)}, u32[]{:S(2)}) collective-permute-start(bf16[1040,128]{1,0:T(8,128)(2,1)S(1)} %shard_map.60.refs_4_), channel_id=1, source_target_pairs={{0,448},{1,449},{2,450},{3,451},{4,452},{5,453},{6,454},{7,455},{8... | collective-permute-start | bytes 798728 | tf_op jit(solution)/shard_map/ppermute | solution.py:58
  41.3 11.3 %collective-permute-start.4 = (bf16[1040,128]{1,0:T(8,128)(2,1)S(1)}, bf16[1040,128]{1,0:T(8,128)(2,1)S(1)}, u32[]{:S(2)}, u32[]{:S(2)}) collective-permute-start(bf16[1040,128]{1,0:T(8,128)(2,1)S(1)} %collective-permute-done.3.refs_4_), channel_id=1, source_target_pairs={{0,64},{1,65},{2,66},{3,67},{4,68},{5,69},{6,70},{7,71},{8,72},{9,... | collective-permute-start | bytes 798728 | tf_op jit(solution)/shard_map/ppermute | solution.py:58
  43.2 10.6 %collective-permute-start.6 = (bf16[1040,128]{1,0:T(8,128)(2,1)S(1)}, bf16[1040,128]{1,0:T(8,128)(2,1)S(1)}, u32[]{:S(2)}, u32[]{:S(2)}) collective-permute-start(bf16[1040,128]{1,0:T(8,128)(2,1)S(1)} %collective-permute-done.5.refs_5_), channel_id=1, source_target_pairs={{0,448},{1,449},{2,450},{3,451},{4,452},{5,453},{6,454},{7,455},{8... | collective-permute-start | bytes 798728 | tf_op jit(solution)/shard_map/ppermute | solution.py:58
  53.8 21.8 %collective-permute-start.7 = (bf16[1040,128]{1,0:T(8,128)(2,1)S(1)}, bf16[1040,128]{1,0:T(8,128)(2,1)S(1)}, u32[]{:S(2)}, u32[]{:S(2)}) collective-permute-start(bf16[1040,128]{1,0:T(8,128)(2,1)S(1)} %broadcast_select_fusion), channel_id=1, source_target_pairs={{0,128},{1,129},{2,130},{3,131},{4,132},{5,133},{6,134},{7,135},{8... | collective-permute-start | bytes 798728 | tf_op jit(solution)/shard_map/ppermute | solution.py:58
  59.4 13.2 %collective-permute-start.8 = (bf16[1040,128]{1,0:T(8,128)(2,1)S(1)}, bf16[1040,128]{1,0:T(8,128)(2,1)S(1)}, u32[]{:S(2)}, u32[]{:S(2)}) collective-permute-start(bf16[1040,128]{1,0:T(8,128)(2,1)S(1)} %collective-permute-done.4.refs_4_), channel_id=1, source_target_pairs={{0,64},{1,65},{2,66},{3,67},{4,68},{5,69},{6,70},{7,71},{8,72},{9,... | collective-permute-start | bytes 798728 | tf_op jit(solution)/shard_map/ppermute | solution.py:58
  64.3 8.3 %collective-permute-start.9 = (bf16[1040,128]{1,0:T(8,128)(2,1)S(1)}, bf16[1040,128]{1,0:T(8,128)(2,1)S(1)}, u32[]{:S(2)}, u32[]{:S(2)}) collective-permute-start(bf16[1040,128]{1,0:T(8,128)(2,1)S(1)} %collective-permute-done.6.refs_5_), channel_id=1, source_target_pairs={{0,448},{1,449},{2,450},{3,451},{4,452},{5,453},{6,454},{7,455},{8... | collective-permute-start | bytes 798728 | tf_op jit(solution)/shard_map/ppermute | solution.py:58
